TPU v7x, 32 devices: a whole 2x2x4 slice. The times are simulated.
32 devices in a mesh: dp: 4 (over z), seq: 8 (over y, x, core).
Axes of the slice: x: 2, y: 2, z: 4, core: 2. Of those that a mesh axis runs over, the one named last changes fastest.
Arguments:
- hidden_in: bfloat16 [8, 1024, 2048], P('dp', 'seq'), may hold values from -6 to 6
- w_qkv: float32 [2048, 1920], P(('dp', 'seq')), may hold values from -0.125 to 0.125
- w_out: float32 [1280, 2048], P(('dp', 'seq')), may hold values from -1.25 to 1.25
- w_gate_up: float32 [2048, 16384], P(('dp', 'seq')), may hold values from -0.125 to 0.125
- w_down: float32 [8192, 2048], P(('dp', 'seq')), may hold values from -0.0625 to 0.0625
- norm_gains: float32 [4224], P(('dp', 'seq')), may hold values from 0.25 to 1.75
- segment_ids: int32 [8, 1024], P('dp', 'seq'), may hold values from 0 to 7, as said below
- positions: int32 [8, 1024], P('dp', 'seq'), may hold values from 0 to 1023, as said below
- out_grad: bfloat16 [8, 1024, 2048], P('dp', 'seq'), may hold values from -6 to 6
Outputs:
- block_out: bfloat16 [8, 1024, 2048], P('dp', 'seq')
- in_grad: bfloat16 [8, 1024, 2048], P('dp', 'seq')
- grad_qkv: float32 [2048, 1920], P(('dp', 'seq'))
- grad_out: float32 [1280, 2048], P(('dp', 'seq'))
- grad_gate_up: float32 [2048, 16384], P(('dp', 'seq'))
- grad_down: float32 [8192, 2048], P(('dp', 'seq'))
- grad_gains: float32 [4224], P(('dp', 'seq'))
Inputs may be any that keep to these rules, and one draw needn't show every extreme that they name: `segment_ids`: in each row the ids start at 0, never fall, and rise by one where a document starts; row 0 is a single document, every other row holds exactly 8 documents. `positions`: A token's position is its distance from the first token of its document in the row.
All inputs are finite; a program needn't handle non-finite values.
Results may differ from a plain program's by a relative error of at most 0.015.
The roundings to bfloat16 on the way count: a program that leaves them out, or rounds other values in their place, can miss the bound.
Values may be sent and summed in bfloat16 or wider, within the bound.
A program may use at most 448 MiB of HBM per device.

v0:
```python
import jax
import jax.numpy as jnp
from jax import lax
from jax.sharding import PartitionSpec as P

D = 2048
QUERY_HEADS = 20
KEY_VALUE_HEADS = 5
HEAD_SIZE = 64
FF = 8192


EPSILON = 1e-06
MASKED = -1e30


def normalized_rows(values):
    scale_rows = lax.rsqrt(jnp.mean(values * values, axis=-1, keepdims=True) + EPSILON)
    return (values * scale_rows, scale_rows)


def normalized_gradient(upstream, unit_vals, scale_rows):
    return scale_rows * (
        upstream - unit_vals * jnp.mean(upstream * unit_vals, axis=-1, keepdims=True)
    )


def apply_rotation(values, cosine_table, sine_table):
    half_dim = values.shape[-1] // 2
    first, second = (values[..., :half_dim], values[..., half_dim:])
    return jnp.concatenate(
        [first * cosine_table - second * sine_table, second * cosine_table + first * sine_table],
        axis=-1,
    )


def rope_tables(position_flat):
    freq = 1.0 / 10000.0 ** (jnp.arange(0, HEAD_SIZE, 2).astype(jnp.float32) / HEAD_SIZE)
    angle = position_flat.astype(jnp.float32)[:, None] * freq[None, :]
    return (jnp.cos(angle)[:, None, :], jnp.sin(angle)[:, None, :])


def contract_rows(left, right):
    return lax.dot_general(
        left, right, (((0,), (0,)), ((), ())), preferred_element_type=jnp.float32
    )


def contract_cols(left, right):
    return lax.dot_general(
        left, right, (((1,), (1,)), ((), ())), preferred_element_type=jnp.float32
    )


def key_blocks(key_value_full, count_of_rows, sequence_length):
    model_width = KEY_VALUE_HEADS * HEAD_SIZE
    key_portion = (
        key_value_full[..., :model_width]
        .reshape(count_of_rows, sequence_length, KEY_VALUE_HEADS, HEAD_SIZE)
        .transpose(0, 2, 1, 3)
    )
    value_portion = (
        key_value_full[..., model_width:]
        .reshape(count_of_rows, sequence_length, KEY_VALUE_HEADS, HEAD_SIZE)
        .transpose(0, 2, 1, 3)
    )
    return (
        key_portion.reshape(count_of_rows * KEY_VALUE_HEADS, sequence_length, HEAD_SIZE),
        value_portion.reshape(count_of_rows * KEY_VALUE_HEADS, sequence_length, HEAD_SIZE),
    )


def swiglu_back(d_hidden, gate_part, up_part, sigmoid_gate, silu_gate):
    d_gate = d_hidden * up_part * sigmoid_gate * (1.0 + gate_part * (1.0 - sigmoid_gate))
    d_up = d_hidden * silu_gate
    return jnp.concatenate([d_gate, d_up], axis=-1).astype(jnp.bfloat16)


def per_device(
    hidden_in, w_qkv, w_out, w_gate_up, w_down, norm_gains, segment_ids, positions, out_grad
):
    count_of_rows, extent_width = (hidden_in.shape[0], hidden_in.shape[1])
    seq_count = lax.axis_size("seq")
    sequence_length = extent_width * seq_count
    token_rows = count_of_rows * extent_width
    query_group = QUERY_HEADS // KEY_VALUE_HEADS
    scale = HEAD_SIZE ** (-0.5)
    query_index = lax.axis_index("seq") * extent_width + jnp.arange(extent_width)
    key_index = jnp.arange(sequence_length)
    w_query, w_proj, gains_low = (
        lax.all_gather(w_qkv.astype(jnp.bfloat16), ("dp", "seq"), axis=0, tiled=True),
        lax.all_gather(w_out.astype(jnp.bfloat16), ("dp", "seq"), axis=0, tiled=True),
        lax.all_gather(norm_gains.astype(jnp.bfloat16), ("dp", "seq"), axis=0, tiled=True),
    )
    gains = gains_low.astype(jnp.float32)
    gain_one = gains[:D]
    gain_two = gains[D : 2 * D]
    gain_query = gains[2 * D : 2 * D + HEAD_SIZE]
    key_gain_vector = gains[2 * D + HEAD_SIZE :]
    inputs = hidden_in.reshape(token_rows, D).astype(jnp.float32)
    x_unit, x_scale = normalized_rows(inputs)
    normed = (x_unit * gain_one).astype(jnp.bfloat16)
    query_key_value_output = jnp.dot(normed, w_query, preferred_element_type=jnp.float32)
    cosine_table, sine_table = rope_tables(positions.reshape(token_rows))
    q_unit, q_scale = normalized_rows(
        query_key_value_output[:, : QUERY_HEADS * HEAD_SIZE].reshape(
            token_rows, QUERY_HEADS, HEAD_SIZE
        )
    )
    key_unit_rows, key_scale = normalized_rows(
        query_key_value_output[
            :, QUERY_HEADS * HEAD_SIZE : (QUERY_HEADS + KEY_VALUE_HEADS) * HEAD_SIZE
        ].reshape(token_rows, KEY_VALUE_HEADS, HEAD_SIZE)
    )
    query_reduced = apply_rotation(q_unit * gain_query, cosine_table, sine_table).astype(
        jnp.bfloat16
    )
    rotated_key = apply_rotation(key_unit_rows * key_gain_vector, cosine_table, sine_table).reshape(
        token_rows, KEY_VALUE_HEADS * HEAD_SIZE
    )
    kv_low = (
        jnp.concatenate(
            [rotated_key, query_key_value_output[:, (QUERY_HEADS + KEY_VALUE_HEADS) * HEAD_SIZE :]],
            axis=-1,
        )
        .astype(jnp.bfloat16)
        .reshape(count_of_rows, extent_width, 2 * KEY_VALUE_HEADS * HEAD_SIZE)
    )
    document_labels = jnp.stack([segment_ids % 128, segment_ids // 128], axis=-1).astype(
        jnp.bfloat16
    )
    key_value_full, key_labels = (
        lax.all_gather(kv_low, "seq", axis=1, tiled=True),
        lax.all_gather(document_labels, "seq", axis=1, tiled=True),
    )
    key_part, value_part = key_blocks(key_value_full, count_of_rows, sequence_length)
    query_blocks = (
        query_reduced.reshape(count_of_rows, extent_width, KEY_VALUE_HEADS, query_group, HEAD_SIZE)
        .transpose(0, 2, 3, 1, 4)
        .reshape(count_of_rows * KEY_VALUE_HEADS, query_group, extent_width, HEAD_SIZE)
    )
    query_label_blocks = jnp.repeat(document_labels, KEY_VALUE_HEADS, axis=0)
    key_label_blocks = jnp.repeat(key_labels, KEY_VALUE_HEADS, axis=0)

    def masked_scores(q_block, k_block, q_dig, k_dig):
        same_doc = (q_dig[:, None, 0] == k_dig[None, :, 0]) & (
            q_dig[:, None, 1] == k_dig[None, :, 1]
        )
        allowed = same_doc & (query_index[:, None] >= key_index[None, :])
        scores = (
            jnp.einsum("gcd,ld->gcl", q_block, k_block, preferred_element_type=jnp.float32) * scale
        )
        return jnp.where(allowed[None], scores, MASKED)

    def attend(block_args):
        q_block, k_block, v_block, q_dig, k_dig = block_args
        scores = masked_scores(q_block, k_block, q_dig, k_dig)
        row_peak = jnp.max(scores, axis=-1, keepdims=True)
        shifted = jnp.exp(scores - row_peak)
        totals = jnp.sum(shifted, axis=-1, keepdims=True)
        probs = (shifted / totals).astype(jnp.bfloat16)
        result = jnp.einsum("gcl,ld->gcd", probs, v_block, preferred_element_type=jnp.float32)
        return (result, (row_peak + jnp.log(totals))[..., 0])

    head_outputs, log_totals = lax.map(
        attend, (query_blocks, key_part, value_part, query_label_blocks, key_label_blocks)
    )
    attended = (
        head_outputs.reshape(count_of_rows, KEY_VALUE_HEADS, query_group, extent_width, HEAD_SIZE)
        .transpose(0, 3, 1, 2, 4)
        .reshape(token_rows, QUERY_HEADS * HEAD_SIZE)
    )
    attended_low = attended.astype(jnp.bfloat16)
    mixed = inputs + jnp.dot(attended_low, w_proj, preferred_element_type=jnp.float32)
    y_unit, y_scale = normalized_rows(mixed)
    normed_two = (y_unit * gain_two).astype(jnp.bfloat16)
    w_gate, w_drop = (
        lax.all_gather(w_gate_up.astype(jnp.bfloat16), ("dp", "seq"), axis=0, tiled=True),
        lax.all_gather(w_down.astype(jnp.bfloat16), ("dp", "seq"), axis=0, tiled=True),
    )
    gate_up = jnp.dot(normed_two, w_gate, preferred_element_type=jnp.float32)
    gate_part = gate_up[:, :FF]
    up_part = gate_up[:, FF:]
    sigmoid_gate = jax.nn.sigmoid(gate_part)
    silu_gate = gate_part * sigmoid_gate
    hidden = (silu_gate * up_part).astype(jnp.bfloat16)
    result = mixed + jnp.dot(hidden, w_drop, preferred_element_type=jnp.float32)
    block_out = result.astype(jnp.bfloat16).reshape(count_of_rows, extent_width, D)
    grad_low = out_grad.reshape(token_rows, D)
    w_gate_b, w_drop_b = (
        lax.all_gather(w_gate_up.astype(jnp.bfloat16), ("dp", "seq"), axis=0, tiled=True),
        lax.all_gather(w_down.astype(jnp.bfloat16), ("dp", "seq"), axis=0, tiled=True),
    )
    d_hidden = contract_cols(grad_low, w_drop_b)
    piece = hidden
    grad_down = lax.psum_scatter(
        contract_rows(piece, grad_low), ("dp", "seq"), scatter_dimension=0, tiled=True
    )
    d_gate_up = swiglu_back(d_hidden, gate_part, up_part, sigmoid_gate, silu_gate)
    piece = normed_two
    grad_gate_up = lax.psum_scatter(
        contract_rows(piece, d_gate_up), ("dp", "seq"), scatter_dimension=0, tiled=True
    )
    d_normed_two = contract_cols(d_gate_up, w_gate_b)
    d_gain_two = jnp.sum(d_normed_two * y_unit, axis=0)
    d_mixed = grad_low.astype(jnp.float32) + normalized_gradient(
        d_normed_two * gain_two, y_unit, y_scale
    )
    d_mixed_low = d_mixed.astype(jnp.bfloat16)
    w_query_b, w_proj_b, gains_back = (
        lax.all_gather(w_qkv.astype(jnp.bfloat16), ("dp", "seq"), axis=0, tiled=True),
        lax.all_gather(w_out.astype(jnp.bfloat16), ("dp", "seq"), axis=0, tiled=True),
        lax.all_gather(norm_gains.astype(jnp.bfloat16), ("dp", "seq"), axis=0, tiled=True),
    )
    grad_out_term = contract_rows(attended_low, d_mixed_low)
    attended_gradient = contract_cols(d_mixed_low, w_proj_b).astype(jnp.bfloat16)
    d_out_blocks = (
        attended_gradient.reshape(
            count_of_rows, extent_width, KEY_VALUE_HEADS, query_group, HEAD_SIZE
        )
        .transpose(0, 2, 3, 1, 4)
        .reshape(count_of_rows * KEY_VALUE_HEADS, query_group, extent_width, HEAD_SIZE)
    )
    kv_back_all, key_labels_backward = (
        lax.all_gather(kv_low, "seq", axis=1, tiled=True),
        lax.all_gather(document_labels, "seq", axis=1, tiled=True),
    )
    key_back, value_back = key_blocks(kv_back_all, count_of_rows, sequence_length)
    key_label_gradient = jnp.repeat(key_labels_backward, KEY_VALUE_HEADS, axis=0)

    def attend_back(block_args):
        q_block, k_block, v_block, q_dig, k_dig, do_block, lse_block = block_args
        scores = masked_scores(q_block, k_block, q_dig, k_dig)
        probs = jnp.exp(scores - lse_block[..., None])
        d_value = jnp.einsum(
            "gcl,gcd->ld", probs.astype(jnp.bfloat16), do_block, preferred_element_type=jnp.float32
        )
        d_probs = jnp.einsum("gcd,ld->gcl", do_block, v_block, preferred_element_type=jnp.float32)
        d_scores = (probs * (d_probs - jnp.sum(probs * d_probs, axis=-1, keepdims=True))).astype(
            jnp.bfloat16
        )
        d_query = (
            jnp.einsum("gcl,ld->gcd", d_scores, k_block, preferred_element_type=jnp.float32) * scale
        )
        d_key = (
            jnp.einsum("gcl,gcd->ld", d_scores, q_block, preferred_element_type=jnp.float32) * scale
        )
        return (d_query, d_key, d_value)

    query_block_gradient, key_block_gradient, value_block_gradient = lax.map(
        attend_back,
        (
            query_blocks,
            key_back,
            value_back,
            query_label_blocks,
            key_label_gradient,
            d_out_blocks,
            log_totals,
        ),
    )
    d_key_all = (
        key_block_gradient.reshape(count_of_rows, KEY_VALUE_HEADS, sequence_length, HEAD_SIZE)
        .transpose(0, 2, 1, 3)
        .reshape(count_of_rows, sequence_length, KEY_VALUE_HEADS * HEAD_SIZE)
    )
    d_value_all = (
        value_block_gradient.reshape(count_of_rows, KEY_VALUE_HEADS, sequence_length, HEAD_SIZE)
        .transpose(0, 2, 1, 3)
        .reshape(count_of_rows, sequence_length, KEY_VALUE_HEADS * HEAD_SIZE)
    )
    key_value_gradient = lax.psum_scatter(
        jnp.concatenate([d_key_all, d_value_all], axis=-1).astype(jnp.bfloat16),
        "seq",
        scatter_dimension=1,
        tiled=True,
    ).astype(jnp.float32)
    d_query_rot = (
        query_block_gradient.reshape(
            count_of_rows, KEY_VALUE_HEADS, query_group, extent_width, HEAD_SIZE
        )
        .transpose(0, 3, 1, 2, 4)
        .reshape(token_rows, QUERY_HEADS, HEAD_SIZE)
    )
    rotated_key_gradient = key_value_gradient[..., : KEY_VALUE_HEADS * HEAD_SIZE].reshape(
        token_rows, KEY_VALUE_HEADS, HEAD_SIZE
    )
    flat_value_gradient = key_value_gradient[..., KEY_VALUE_HEADS * HEAD_SIZE :].reshape(
        token_rows, KEY_VALUE_HEADS * HEAD_SIZE
    )
    d_query_norm = apply_rotation(d_query_rot, cosine_table, -sine_table)
    key_norm_gradient = apply_rotation(rotated_key_gradient, cosine_table, -sine_table)
    d_gain_query = jnp.sum(d_query_norm * q_unit, axis=(0, 1))
    d_gain_key = jnp.sum(key_norm_gradient * key_unit_rows, axis=(0, 1))
    d_query_raw = normalized_gradient(d_query_norm * gain_query, q_unit, q_scale).reshape(
        token_rows, QUERY_HEADS * HEAD_SIZE
    )
    raw_key_gradient = normalized_gradient(
        key_norm_gradient * key_gain_vector, key_unit_rows, key_scale
    ).reshape(token_rows, KEY_VALUE_HEADS * HEAD_SIZE)
    d_proj_qkv = jnp.concatenate(
        [d_query_raw, raw_key_gradient, flat_value_gradient], axis=-1
    ).astype(jnp.bfloat16)
    grad_qkv_term = contract_rows(normed, d_proj_qkv)
    d_normed = contract_cols(d_proj_qkv, w_query_b)
    d_gain_one = jnp.sum(d_normed * x_unit, axis=0)
    d_inputs = d_mixed + normalized_gradient(d_normed * gain_one, x_unit, x_scale)
    gain_term = jnp.concatenate([d_gain_one, d_gain_two, d_gain_query, d_gain_key])
    grad_qkv, grad_out, grad_gains = (
        lax.psum_scatter(grad_qkv_term, ("dp", "seq"), scatter_dimension=0, tiled=True),
        lax.psum_scatter(grad_out_term, ("dp", "seq"), scatter_dimension=0, tiled=True),
        lax.psum_scatter(gain_term, ("dp", "seq"), scatter_dimension=0, tiled=True),
    )
    in_grad = d_inputs.astype(jnp.bfloat16).reshape(count_of_rows, extent_width, D)
    return (block_out, in_grad, grad_qkv, grad_out, grad_gate_up, grad_down, grad_gains)


def solution(mesh):
    return jax.shard_map(
        per_device,
        mesh=mesh,
        in_specs=(
            P("dp", "seq", None),
            P(("dp", "seq"), None),
            P(("dp", "seq"), None),
            P(("dp", "seq"), None),
            P(("dp", "seq"), None),
            P(("dp", "seq")),
            P("dp", "seq"),
            P("dp", "seq"),
            P("dp", "seq", None),
        ),
        out_specs=(
            P("dp", "seq", None),
            P("dp", "seq", None),
            P(("dp", "seq"), None),
            P(("dp", "seq"), None),
            P(("dp", "seq"), None),
            P(("dp", "seq"), None),
            P(("dp", "seq")),
        ),
        check_vma=False,
    )
```

profile of v0, /device:TPU:14, one launch (start us, length us, event | category | flops | bytes accessed | tf_op | source)
XLA Modules:
  0.0 3420.8 jit_solution(17536805393902361603)
XLA Ops:
  10.0 40.9 %all-reduce = bf16[4224]{0:T(1024)(128)(2,1)S(1)} all-reduce(bf16[4224]{0:T(1024)(128)(2,1)S(1)} %dynamic-update-slice), channel_id=1, replica_groups=mesh['dp'=4,'seq'=8] {'dp','seq'}, use_global_device_ids=true, to_apply=%add | all-reduce | flops 4224 | bytes 16896
  54.4 32.9 all-gather.6.cloned.1.call-done
  87.2 5.6 fusion.79
  103.6 9.0 all_gather.27
  119.6 16.7 all-gather.8.cloned.1.call-done
  156.9 47.9 %while.30 = (s32[]{:T(128)}, bf16[10,4,128,64]{2,3,1,0:T(8,128)(2,1)}, f32[10,4,128]{2,1,0:T(4,128)S(1)}, bf16[10,128,2]{1,2,0:T(2,128)(2,1)S(1)}, bf16[10,1024,...) while((s32[]{:T(128)}, ...), condition=%wide.region_6.7_spmd.clone.clone, body=%wide.region_3.6_spmd.clone.sunk.clone | while | flops 141688448 | bytes 7317109 | solution.py:165
  211.8 348.3 %all-gather.12.cloned.1.call-done = bf16[2048,16384]{1,0:T(8,128)(2,1)} async-done(((bf16[64,16384]{1,0:T(8,128)(2,1)}), bf16[2048,16384]{1,0:T(8,128)(2,1)}) %all-gather.12.cloned.1.call-update) | async-done | bytes 67108880 | tf_op jit(solution)/shard_map/all_gather | solution.py:178
  560.1 33.5 fusion.75
  593.6 162.1 %all-gather.14.cloned.1.call-done = bf16[8192,2048]{1,0:T(8,128)(2,1)} async-done(((bf16[256,2048]{1,0:T(8,128)(2,1)}), bf16[8192,2048]{1,0:T(8,128)(2,1)}) %all-gather.14.cloned.1.call-update) | async-done | bytes 33554448 | tf_op jit(solution)/shard_map/all_gather | solution.py:179
  755.7 23.2 multiply_convert_fusion.2
  778.9 29.6 multiply_reduce_fusion.1
  816.7 86.5 %while.31 = (s32[]{:T(128)}, f32[10,4,128,64]{2,3,1,0:T(8,128)}, bf16[10,1024,64]{1,2,0:T(8,128)(2,1)}, bf16[10,1024,64]{1,2,0:T(8,128)(2,1)}, bf16[10,128,2]{1,...) while((s32[]{:T(128)}, f32[10,4,128,64]{2,3,1,0:T(8,128)}, ...), condition=%wide.region_11.12_spmd.clone.clone, body=%wide.region_9.11_spmd.clone.sunk.clone | while | flops 341540480 | bytes 17341068 | solution.py:250
  906.6 7.5 copy.148
  918.9 7.1 fusion.59
  946.0 15.6 reduce-scatter.17.cloned.1.call-done
  970.0 9.0 fusion.80
  980.3 26.0 fusion.81
  1006.4 48.3 %fusion.56 = f32[2048,16384]{1,0:T(8,128)} fusion(bf16[256,8192]{1,0:T(8,128)(2,1)} %get-tuple-element.348, bf16[256,8192]{1,0:T(8,128)(2,1)} %get-tuple-element.347, f32[256,2048]{1,0:T(8,128)S(1)} %get-tuple-element.388, f32[2048]{0:T(1024)S(1)} %get-tuple-element.378, f32[256]{0:T(256)S(1)} %add_rsqrt_fusion.2), kind=kOutput, calls=%fused_computation.85 | convolution fusion | flops 17198219264 | bytes 144712704 | tf_op jit(solution)/shard_map/dot_general | solution.py:44
  1054.9 17.5 fusion.58
  1072.7 7.5 multiply_reduce_fusion.2
  1080.2 42.7 %all-reduce.2 = f32[4224]{0:T(1024)S(1)} all-reduce(f32[4224]{0:T(1024)S(1)} %concatenate.69), channel_id=7, replica_groups=mesh['dp'=4,'seq'=8] {'dp','seq'}, use_global_device_ids=true, to_apply=%region_26.27.clone | all-reduce | flops 4224 | bytes 33792
  1126.8 164.9 %reduce-scatter.11.cloned.1.call-done = f32[64,1920]{1,0:T(8,128)} async-done(((f32[2048,1920]{1,0:T(8,128)}), f32[64,1920]{1,0:T(8,128)}) %reduce-scatter.11.cloned.1.call-update) | async-done | bytes 491536 | tf_op jit(solution)/shard_map/reduce_scatter | solution.py:310
  1291.6 712.0 %reduce-scatter.15.cloned.1.call-done = f32[256,2048]{1,0:T(8,128)} async-done(((f32[8192,2048]{1,0:T(8,128)}), f32[256,2048]{1,0:T(8,128)}) %reduce-scatter.15.cloned.1.call-update) | async-done | bytes 2097168 | tf_op jit(solution)/shard_map/reduce_scatter | solution.py:196
  2003.7 1409.8 %reduce-scatter.19.cloned.1.call-done = f32[64,16384]{1,0:T(8,128)} async-done(((f32[2048,16384]{1,0:T(8,128)}), f32[64,16384]{1,0:T(8,128)}) %reduce-scatter.19.cloned.1.call-update) | async-done | bytes 4194320
  (431 shorter events, 235.0 us)
Async XLA Ops:
  7.2 46.9 %copy-start.4 = (bf16[2,128,2048]{2,1,0:T(8,128)(2,1)S(1)}, bf16[2,128,2048]{2,1,0:T(8,128)(2,1)}, u32[]{:S(2)}) copy-start(bf16[2,128,2048]{2,1,0:T(8,128)(2,1)} %param.13) | copy-start | bytes 3145732
  7.2 80.0 %all-gather.6.cloned.1.call-start = ((), (), s32[]{:S(2)}) async-start(), calls=%async_computation.5 | async-start | bytes 8110080 | tf_op jit(solution)/shard_map/all_gather | solution.py:91
  9.1 127.2 %all-gather.8.cloned.1.call-start = ((), (), s32[]{:S(2)}) async-start(), calls=%async_computation.6 | async-start | bytes 2949120 | tf_op jit(solution)/shard_map/all_gather | solution.py:133
  52.4 40.3 %copy-start.30 = (f32[256]{0:T(256)}, f32[256]{0:T(256)S(1)}, u32[]{:S(2)}) copy-start(f32[256]{0:T(256)S(1)} %rsqrt_bitcast_fusion) | copy-start | bytes 3076
  53.2 41.4 %copy-start.32 = (f32[64]{0:T(128)}, f32[64]{0:T(128)S(1)}, u32[]{:S(2)}) copy-start(f32[64]{0:T(128)S(1)} %get-tuple-element.380) | copy-start | bytes 772
  53.2 63.5 %copy-start.35 = (f32[64]{0:T(128)}, f32[64]{0:T(128)S(1)}, u32[]{:S(2)}) copy-start(f32[64]{0:T(128)S(1)} %get-tuple-element.381) | copy-start | bytes 772
  53.2 39.6 %copy-start.28 = (f32[2048]{0:T(1024)}, f32[2048]{0:T(1024)S(1)}, u32[]{:S(2)}) copy-start(f32[2048]{0:T(1024)S(1)} %get-tuple-element.379) | copy-start | bytes 24580
  54.0 63.0 %copy-start.20 = (f32[256,32]{0,1:T(8,128)}, f32[256,32]{0,1:T(8,128)S(1)}, u32[]{:S(2)}) copy-start(f32[256,32]{0,1:T(8,128)S(1)} %get-tuple-element.384) | copy-start | bytes 98308
  54.3 38.5 %copy-start.13 = (bf16[256,2048]{1,0:T(8,128)(2,1)}, bf16[256,2048]{1,0:T(8,128)(2,1)S(1)}, u32[]{:S(2)}) copy-start(bf16[256,2048]{1,0:T(8,128)(2,1)S(1)} %multiply_convert_fusion.5) | copy-start | bytes 3145732
  96.0 111.5 %all-gather.10.cloned.1.call-start = ((), (), s32[]{:S(2)}) async-start(), calls=%async_computation.7 | async-start | bytes 5406720 | tf_op jit(solution)/shard_map/all_gather | solution.py:92
  96.7 463.4 %all-gather.12.cloned.1.call-start = ((), (), s32[]{:S(2)}) async-start(), calls=%async_computation.8 | async-start | bytes 69206016 | tf_op jit(solution)/shard_map/all_gather | solution.py:178
  100.5 655.2 %all-gather.14.cloned.1.call-start = ((), (), s32[]{:S(2)}) async-start(), calls=%async_computation.9 | async-start | bytes 34603008 | tf_op jit(solution)/shard_map/all_gather | solution.py:179
  103.5 858.1 %reduce-scatter.17.cloned.1.call-start = ((), (), s32[]{:S(2)}) async-start(), calls=%async_computation.13 | async-start | bytes 2949120
  560.1 195.6 %copy-start.11 = (bf16[2,128,2048]{2,1,0:T(8,128)(2,1)S(1)}, bf16[2,128,2048]{2,1,0:T(8,128)(2,1)}, u32[]{:S(2)}) copy-start(bf16[2,128,2048]{2,1,0:T(8,128)(2,1)} %param.21) | copy-start | bytes 3145732
  917.8 208.9 %reduce-scatter.13.cloned.1.call-start = ((), (), s32[]{:S(2)}) async-start(), calls=%async_computation.11 | async-start | bytes 10813440 | tf_op jit(solution)/shard_map/reduce_scatter | solution.py:311
  926.0 365.7 %reduce-scatter.11.cloned.1.call-start = ((), (), s32[]{:S(2)}) async-start(), calls=%async_computation.10 | async-start | bytes 16220160 | tf_op jit(solution)/shard_map/reduce_scatter | solution.py:310
  946.0 18.3 copy-start.8
  946.0 18.3 copy-start.27
  979.1 1024.6 %reduce-scatter.15.cloned.1.call-start = ((), (), s32[]{:S(2)}) async-start(), calls=%async_computation.12 | async-start | bytes 69206016 | tf_op jit(solution)/shard_map/reduce_scatter | solution.py:196
  1006.4 2407.1 %reduce-scatter.19.cloned.1.call-start = ((), (), s32[]{:S(2)}) async-start(), calls=%async_computation.14 | async-start | bytes 138412032
  1054.9 17.8 copy-start.5
  1054.9 17.7 copy-start.29
  1054.9 17.7 copy-start.31
  1072.7 50.9 %copy-start.3 = (f32[256,2048]{1,0:T(8,128)S(1)}, f32[256,2048]{1,0:T(8,128)}, u32[]{:S(2)}) copy-start(f32[256,2048]{1,0:T(8,128)} %copy-done.2) | copy-start | bytes 6291460
  (24 other events, 108.5 us)
Sparse Core Ops, SparseCore 0:
  11.5 75.7 all-gather.5
  96.1 40.1 all-gather.7
  139.1 65.3 all-gather.9
  207.8 352.2 all-gather.11
  563.4 192.3 all-gather.13
  918.0 43.5 reduce-scatter.16
  964.4 131.0 reduce-scatter.12
  1102.1 189.5 reduce-scatter.10
  1294.6 709.0 reduce-scatter.14
  2006.5 1406.9 reduce-scatter.18
where the time goes:
time: 3430 us; the launch traced here: 3420 us
  waiting for transfers between devices  2860 us (83%)
  matrix products  334 us (10%)
  blocking collectives  92.6 us (3%)
  local copies, waits for them, and re-layouts  67.5 us (2%)
  other arithmetic  47.2 us (1%)
    unnamed x12, waiting for transfers between devices  1430 us
    reduce_scatter x1, waiting for transfers between devices, per_device(): lax.psum_scatter(contract_rows(piece, grad_low), ('dp', 'seq'), scatter_d...  712 us
    all_gather x1, waiting for transfers between devices, per_device(): lax.all_gather(w_gate_up.astype(jnp.bfloat16), ('dp', 'seq'), axis=0, til...  348 us
    reduce_scatter x1, waiting for transfers between devices, per_device(): lax.psum_scatter(grad_qkv_term, ('dp', 'seq'), scatter_dimension=0, tiled...  165 us
    all_gather x1, waiting for transfers between devices, per_device(): lax.all_gather(w_down.astype(jnp.bfloat16), ('dp', 'seq'), axis=0, tiled=...  162 us
    dot_general x4, matrix products, contract_rows(): lax.dot_general(left, right, (((0,), (0,)), ((), ())), preferred_element_...  90.5 us
    unnamed x2, blocking collectives  83.6 us
  transfers between devices with their start and end apart: 10, of which 8 were waited for; matrix products, arithmetic and copies ran while one was open for 8% of the time, Pallas kernels for 0%

commit v1 on v0

v1 whole, which is shorter than its diff:
```python
import functools

import jax
import jax.numpy as jnp
from jax import lax
from jax.experimental import pallas as pl
from jax.experimental.pallas import tpu as pltpu
from jax.sharding import PartitionSpec as P

D = 2048
QUERY_HEADS = 20
KEY_VALUE_HEADS = 5
HEAD_SIZE = 64
FF = 8192
GROUP = QUERY_HEADS // KEY_VALUE_HEADS
QUERY_WIDTH = QUERY_HEADS * HEAD_SIZE
PAIR_WIDTH = 2 * HEAD_SIZE
KV_WIDTH = KEY_VALUE_HEADS * PAIR_WIDTH
GROUP_WIDTH = GROUP * HEAD_SIZE

EPSILON = 1e-06
MASKED = -1e30
SCALE = HEAD_SIZE ** (-0.5)


def normalized_rows(values):
    scale_rows = lax.rsqrt(jnp.mean(values * values, axis=-1, keepdims=True) + EPSILON)
    return (values * scale_rows, scale_rows)


def normalized_gradient(upstream, unit_vals, scale_rows):
    return scale_rows * (
        upstream - unit_vals * jnp.mean(upstream * unit_vals, axis=-1, keepdims=True)
    )


def apply_rotation(values, cosine_table, sine_table):
    half_dim = values.shape[-1] // 2
    first, second = (values[..., :half_dim], values[..., half_dim:])
    return jnp.concatenate(
        [first * cosine_table - second * sine_table, second * cosine_table + first * sine_table],
        axis=-1,
    )


def rope_tables(position_flat):
    freq = 1.0 / 10000.0 ** (jnp.arange(0, HEAD_SIZE, 2).astype(jnp.float32) / HEAD_SIZE)
    angle = position_flat.astype(jnp.float32)[:, None] * freq[None, :]
    return (jnp.cos(angle)[:, None, :], jnp.sin(angle)[:, None, :])


def matmul(left, right):
    return jnp.dot(left, right, preferred_element_type=jnp.float32)


def contract_rows(left, right):
    return lax.dot_general(
        left, right, (((0,), (0,)), ((), ())), preferred_element_type=jnp.float32
    )


def contract_cols(left, right):
    return lax.dot_general(
        left, right, (((1,), (1,)), ((), ())), preferred_element_type=jnp.float32
    )


def shifted(piece, shift):
    count = lax.axis_size("dp")
    return lax.ppermute(piece, "dp", [(i, (i + shift) % count) for i in range(count)])


def rotate_gather(piece):
    return [piece] + [shifted(piece, s) for s in range(1, lax.axis_size("dp"))]


def rotate_reduce(partial, rows):
    total = partial[:rows].astype(jnp.float32)
    for s in range(1, lax.axis_size("dp")):
        piece = partial[s * rows : (s + 1) * rows].astype(jnp.bfloat16)
        total = total + shifted(piece, -s).astype(jnp.float32)
    return total


def in_order(slots):
    count = len(slots)
    back = slots[::-1] + slots[::-1]
    start = count - 1 - lax.axis_index("dp")
    return lax.dynamic_slice_in_dim(jnp.stack(back[:-1]), start, count, axis=0)


def exchange_blocks(blocks):
    count = lax.axis_size("dp")
    me = lax.axis_index("dp")
    pick = lambda s: lax.dynamic_index_in_dim(blocks, lax.rem(me + s, count), 0, keepdims=False)
    return in_order([pick(0)] + [shifted(pick(s), s) for s in range(1, count)])


def reduce_blocks(blocks):
    count = lax.axis_size("dp")
    me = lax.axis_index("dp")
    pick = lambda s: lax.dynamic_index_in_dim(blocks, lax.rem(me + s, count), 0, keepdims=False)
    total = pick(0).astype(jnp.float32)
    for s in range(1, count):
        total = total + shifted(pick(s), s).astype(jnp.float32)
    return total


def bit_orders(count, ways):
    bits = [1 << i for i in range(1, count.bit_length() - 1)]
    half = (len(bits) + 1) // 2
    low, high = bits[:half], bits[half:]
    orders = []
    for way in range(ways):
        one, two = (low, high) if way % 2 == 0 else (high, low)
        order = []
        for i in range(half):
            order += one[i : i + 1] + two[i : i + 1]
        orders.append(tuple(order + [1]))
    return orders


def crossed(piece, bit):
    count = lax.axis_size("seq")
    return lax.ppermute(piece, "seq", [(i, i ^ bit) for i in range(count)])


def cube_gather(piece, bits):
    for bit in bits:
        piece = jnp.concatenate([piece, crossed(piece, bit)], axis=0)
    return piece


def cube_offsets(bits):
    offsets = [0]
    for bit in bits:
        offsets = offsets + [o ^ bit for o in offsets]
    return tuple(offsets)


def cube_reduce(partial, bits):
    for bit in bits[::-1]:
        half = partial.shape[0] // 2
        partial = partial[:half].astype(jnp.float32) + crossed(
            partial[half:].astype(jnp.bfloat16), bit
        ).astype(jnp.float32)
    return partial


def fill_bias(place_ref, start_ref, bias_ref, offsets):
    rows = start_ref.shape[1]
    place = place_ref[0]
    query = place * rows + lax.broadcasted_iota(jnp.int32, (rows, rows), 1)
    begin = start_ref[...]
    local = lax.broadcasted_iota(jnp.int32, (rows, rows), 0)
    for slot, offset in enumerate(offsets):
        key = (place ^ offset) * rows + local
        allowed = (key <= query) & (key >= begin)
        bias_ref[slot * rows : (slot + 1) * rows, :] = jnp.where(allowed, 0.0, MASKED)


def stacked_heads(block, place):
    rows = block.shape[0]
    turned = block.astype(jnp.float32).T
    heads = jnp.concatenate(
        [turned[g * HEAD_SIZE : (g + 1) * HEAD_SIZE] for g in range(GROUP)], axis=1
    ).astype(jnp.bfloat16)
    empty = jnp.zeros((HEAD_SIZE, GROUP * rows), jnp.bfloat16)
    return jnp.concatenate([heads, empty] if place == 0 else [empty, heads], axis=0)


def unstacked_heads(turned):
    rows = turned.shape[1] // GROUP
    return jnp.concatenate([turned[:, g * rows : (g + 1) * rows] for g in range(GROUP)], axis=0).T


def attend_kernel(offsets, place_ref, start_ref, q_ref, kv_ref, out_ref, lse_ref, bias_ref):
    @pl.when(pl.program_id(0) == 0)
    def _():
        fill_bias(place_ref, start_ref, bias_ref, offsets)

    pairs = kv_ref[...]
    queries = stacked_heads(q_ref[...], 0)
    bias = jnp.concatenate([bias_ref[...]] * GROUP, axis=1)
    scores = matmul(pairs, queries) + bias
    peak = jnp.max(scores, axis=0, keepdims=True)
    raised = jnp.exp(scores - peak)
    totals = jnp.sum(raised, axis=0, keepdims=True)
    probs = (raised * (1.0 / totals)).astype(jnp.bfloat16)
    mixed = contract_rows(pairs, probs)
    out_ref[...] = unstacked_heads(mixed[HEAD_SIZE:]).astype(jnp.bfloat16)
    lse_ref[0] = peak + jnp.log(totals)


def attend_back_kernel(
    offsets, place_ref, start_ref, q_ref, kv_ref, do_ref, lse_ref, dq_ref, dkv_ref, bias_ref
):
    @pl.when(pl.program_id(0) == 0)
    def _():
        fill_bias(place_ref, start_ref, bias_ref, offsets)

    pairs = kv_ref[...]
    queries = stacked_heads(q_ref[...], 0)
    upstream = stacked_heads(do_ref[...], 1)
    bias = jnp.concatenate([bias_ref[...]] * GROUP, axis=1)
    probs = jnp.exp(matmul(pairs, queries) + bias - lse_ref[0])
    d_probs = matmul(pairs, upstream)
    center = jnp.sum(probs * d_probs, axis=0, keepdims=True)
    d_scores = (probs * (d_probs - center)).astype(jnp.bfloat16)
    d_pairs = contract_cols(d_scores, queries) + contract_cols(
        probs.astype(jnp.bfloat16), upstream
    )
    dkv_ref[...] = d_pairs.astype(jnp.bfloat16)
    d_queries = contract_rows(pairs, d_scores)
    dq_ref[...] = unstacked_heads(d_queries[:HEAD_SIZE]) * SCALE


def row_specs(rows, keys):
    place = pl.BlockSpec(memory_space=pltpu.SMEM)
    start = pl.BlockSpec((1, rows), lambda h: (0, 0))
    heads = pl.BlockSpec((rows, GROUP_WIDTH), lambda h: (0, h))
    pairs = pl.BlockSpec((keys, PAIR_WIDTH), lambda h: (0, h))
    lse = pl.BlockSpec((1, 1, GROUP * rows), lambda h: (h, 0, 0))
    return place, start, heads, pairs, lse


def attend(offsets, place, start, queries, pairs):
    rows, keys = queries.shape[0], pairs.shape[0]
    at, begin, heads, blocks, lse = row_specs(rows, keys)
    return pl.pallas_call(
        functools.partial(attend_kernel, offsets),
        grid=(KEY_VALUE_HEADS,),
        in_specs=[at, begin, heads, blocks],
        out_specs=[heads, lse],
        out_shape=[
            jax.ShapeDtypeStruct((rows, QUERY_WIDTH), jnp.bfloat16),
            jax.ShapeDtypeStruct((KEY_VALUE_HEADS, 1, GROUP * rows), jnp.float32),
        ],
        scratch_shapes=[pltpu.VMEM((keys, rows), jnp.float32)],
        cost_estimate=pl.CostEstimate(
            flops=8 * rows * keys * QUERY_WIDTH,
            bytes_accessed=4 * rows * QUERY_WIDTH + 2 * keys * KV_WIDTH,
            transcendentals=rows * keys * QUERY_HEADS,
        ),
    )(place, start, queries, pairs)


def attend_back(offsets, place, start, queries, pairs, upstream, lse_rows):
    rows, keys = queries.shape[0], pairs.shape[0]
    at, begin, heads, blocks, lse = row_specs(rows, keys)
    return pl.pallas_call(
        functools.partial(attend_back_kernel, offsets),
        grid=(KEY_VALUE_HEADS,),
        in_specs=[at, begin, heads, blocks, heads, lse],
        out_specs=[heads, blocks],
        out_shape=[
            jax.ShapeDtypeStruct((rows, QUERY_WIDTH), jnp.float32),
            jax.ShapeDtypeStruct((keys, KV_WIDTH), jnp.bfloat16),
        ],
        scratch_shapes=[pltpu.VMEM((keys, rows), jnp.float32)],
        cost_estimate=pl.CostEstimate(
            flops=20 * rows * keys * QUERY_WIDTH,
            bytes_accessed=8 * rows * QUERY_WIDTH + 4 * keys * KV_WIDTH,
            transcendentals=rows * keys * QUERY_HEADS,
        ),
    )(place, start, queries, pairs, upstream, lse_rows)


def paired(columns):
    rows = columns.shape[0]
    return (
        columns.reshape(rows, 2, KEY_VALUE_HEADS, HEAD_SIZE)
        .transpose(0, 2, 1, 3)
        .reshape(rows, KV_WIDTH)
    )


def unpaired(columns):
    rows = columns.shape[0]
    return (
        columns.reshape(rows, KEY_VALUE_HEADS, 2, HEAD_SIZE)
        .transpose(0, 2, 1, 3)
        .reshape(rows, KV_WIDTH)
    )


def per_device(
    hidden_in, w_qkv, w_out, w_gate_up, w_down, norm_gains, segment_ids, positions, out_grad
):
    row_count, rows = (hidden_in.shape[0], hidden_in.shape[1])
    dp_count, seq_count = (lax.axis_size("dp"), lax.axis_size("seq"))
    tokens = row_count * rows
    ff_part = FF // dp_count
    place = lax.axis_index("seq")
    orders = bit_orders(seq_count, row_count)
    low = jnp.bfloat16
    split = lambda array: [array[r * rows : (r + 1) * rows] for r in range(row_count)]

    here = place * rows + jnp.arange(rows, dtype=jnp.int32)
    starts = (here[None, :] - positions).reshape(row_count, 1, rows)
    place_one = place.astype(jnp.int32).reshape(1)

    with jax.named_scope("gather_qkv"):
        qkv_low = jnp.concatenate(
            [w_qkv[:, :QUERY_WIDTH], paired(w_qkv[:, QUERY_WIDTH:])], axis=1
        ).astype(low)
        w_query = lax.all_gather(qkv_low, ("dp", "seq"), axis=0, tiled=True)
    with jax.named_scope("gather_gains"):
        gains = lax.all_gather(
            norm_gains.astype(low), ("dp", "seq"), axis=0, tiled=True
        ).astype(jnp.float32)
    with jax.named_scope("swap_gate"):
        gate_rows = w_gate_up.shape[0]
        gate_blocks = (
            w_gate_up.astype(low)
            .reshape(gate_rows, 2, dp_count, ff_part)
            .transpose(2, 0, 1, 3)
            .reshape(dp_count, gate_rows, 2 * ff_part)
        )
        gate_cols = exchange_blocks(gate_blocks)
    with jax.named_scope("swap_out"):
        proj_rows = in_order(rotate_gather(w_out.astype(low)))
    with jax.named_scope("gather_out"):
        w_proj = lax.all_gather(proj_rows, "seq", axis=1, tiled=True).reshape(QUERY_WIDTH, D)
    with jax.named_scope("gather_gate"):
        w_gate = lax.all_gather(gate_cols, "seq", axis=1, tiled=True).reshape(D, 2 * ff_part)
    with jax.named_scope("gather_down"):
        w_drop = lax.all_gather(w_down.astype(low), "seq", axis=0, tiled=True)
    grad_low = out_grad.reshape(tokens, D)
    with jax.named_scope("swap_grad"):
        grad_all = [jnp.concatenate(rotate_gather(g), axis=0) for g in split(grad_low)]

    gain_one = gains[:D]
    gain_two = gains[D : 2 * D]
    gain_query = gains[2 * D : 2 * D + HEAD_SIZE]
    gain_key = gains[2 * D + HEAD_SIZE :]
    inputs = hidden_in.reshape(tokens, D).astype(jnp.float32)
    x_unit, x_scale = normalized_rows(inputs)
    normed = (x_unit * gain_one).astype(low)
    with jax.named_scope("project_qkv"):
        qkv = matmul(normed, w_query)
    cosine, sine = rope_tables(positions.reshape(tokens))
    q_unit, q_scale = normalized_rows(
        qkv[:, :QUERY_WIDTH].reshape(tokens, QUERY_HEADS, HEAD_SIZE)
    )
    kv_heads = qkv[:, QUERY_WIDTH:].reshape(tokens, KEY_VALUE_HEADS, PAIR_WIDTH)
    k_unit, k_scale = normalized_rows(kv_heads[..., :HEAD_SIZE])
    queries = apply_rotation(q_unit * gain_query, cosine, sine).astype(low).reshape(
        tokens, QUERY_WIDTH
    ) * jnp.asarray(SCALE, low)
    keys = apply_rotation(k_unit * gain_key, cosine, sine)
    kv_low = (
        jnp.concatenate([keys, kv_heads[..., HEAD_SIZE:]], axis=-1)
        .astype(low)
        .reshape(tokens, KV_WIDTH)
    )

    attended, lse, pairs, mixed, normed_two, y_unit, y_scale, normed_all = ([] for _ in range(8))
    query_rows, kv_rows, input_rows = split(queries), split(kv_low), split(inputs)
    for r in range(row_count):
        with jax.named_scope(f"gather_kv{r}"):
            pairs.append(cube_gather(kv_rows[r], orders[r]))
    for r in range(row_count):
        with jax.named_scope(f"attend{r}"):
            out_r, lse_r = attend(
                cube_offsets(orders[r]), place_one, starts[r], query_rows[r], pairs[r]
            )
        attended.append(out_r)
        lse.append(lse_r)
        with jax.named_scope(f"project_out{r}"):
            mixed.append(input_rows[r] + matmul(out_r, w_proj))
        unit_r, scale_r = normalized_rows(mixed[r])
        y_unit.append(unit_r)
        y_scale.append(scale_r)
        normed_two.append((unit_r * gain_two).astype(low))
        with jax.named_scope(f"swap_normed{r}"):
            normed_all.append(jnp.concatenate(rotate_gather(normed_two[r]), axis=0))

    hidden, d_gate_up, d_normed, block_rows = ([] for _ in range(4))
    for r in range(row_count):
        with jax.named_scope(f"back_down{r}"):
            d_hidden = contract_cols(grad_all[r], w_drop)
        with jax.named_scope(f"gate_up{r}"):
            gate_up = matmul(normed_all[r], w_gate)
        gate, up = gate_up[:, :ff_part], gate_up[:, ff_part:]
        sigmoid_gate = jax.nn.sigmoid(gate)
        silu_gate = gate * sigmoid_gate
        hidden.append((silu_gate * up).astype(low))
        d_gate = d_hidden * up * sigmoid_gate * (1.0 + gate * (1.0 - sigmoid_gate))
        d_gate_up.append(jnp.concatenate([d_gate, d_hidden * silu_gate], axis=-1).astype(low))
        with jax.named_scope(f"back_gate{r}"):
            d_partial = contract_cols(d_gate_up[r], w_gate).astype(low)
        with jax.named_scope(f"reduce_normed{r}"):
            d_normed.append(rotate_reduce(d_partial, rows))
    for r in range(row_count):
        with jax.named_scope(f"down{r}"):
            y_partial = matmul(hidden[r], w_drop).astype(low)
        with jax.named_scope(f"reduce_down{r}"):
            block_rows.append((mixed[r] + rotate_reduce(y_partial, rows)).astype(low))
    block_out = jnp.stack(block_rows)

    join = lambda parts: jnp.concatenate(parts, axis=0)
    with jax.named_scope("grad_gate"):
        gate_term = contract_rows(join(normed_all), join(d_gate_up)).astype(low)
    with jax.named_scope("grad_down"):
        down_term = contract_rows(join(hidden), join(grad_all)).astype(low)
    gate_term, down_term, *d_normed = lax.optimization_barrier((gate_term, down_term, *d_normed))
    with jax.named_scope("scatter_gate"):
        gate_sum = lax.psum_scatter(
            gate_term.reshape(dp_count, D // dp_count, 2 * ff_part),
            "seq", scatter_dimension=1, tiled=True,
        )
    with jax.named_scope("scatter_down"):
        grad_down = lax.psum_scatter(
            down_term, "seq", scatter_dimension=0, tiled=True
        ).astype(jnp.float32)
    with jax.named_scope("return_gate"):
        grad_gate_up = (
            exchange_blocks(gate_sum)
            .reshape(dp_count, gate_rows, 2, ff_part)
            .transpose(1, 2, 0, 3)
            .reshape(gate_rows, 2 * FF)
            .astype(jnp.float32)
        )

    d_mixed, d_mixed_low, d_queries, d_kv = ([] for _ in range(4))
    grad_rows = split(grad_low)
    d_gain_two = 0.0
    for r in range(row_count):
        d_gain_two = d_gain_two + jnp.sum(d_normed[r] * y_unit[r], axis=0)
        d_mixed.append(
            grad_rows[r].astype(jnp.float32)
            + normalized_gradient(d_normed[r] * gain_two, y_unit[r], y_scale[r])
        )
        d_mixed_low.append(d_mixed[r].astype(low))
        with jax.named_scope(f"back_out{r}"):
            d_attended = contract_cols(d_mixed_low[r], w_proj).astype(low)
        with jax.named_scope(f"attend_back{r}"):
            dq_r, dkv_r = attend_back(
                cube_offsets(orders[r]), place_one, starts[r], query_rows[r], pairs[r],
                d_attended, lse[r],
            )
        d_queries.append(dq_r)
        with jax.named_scope(f"reduce_kv{r}"):
            d_kv.append(cube_reduce(dkv_r, orders[r]))
    with jax.named_scope("grad_out"):
        out_term = contract_rows(join(attended), join(d_mixed_low)).astype(low)
    with jax.named_scope("scatter_out"):
        out_sum = lax.psum_scatter(
            out_term.reshape(dp_count, QUERY_WIDTH // dp_count, D),
            "seq", scatter_dimension=1, tiled=True,
        )
    with jax.named_scope("return_out"):
        grad_out = reduce_blocks(out_sum)

    d_q = apply_rotation(
        join(d_queries).reshape(tokens, QUERY_HEADS, HEAD_SIZE), cosine, -sine
    )
    d_pairs = join(d_kv).reshape(tokens, KEY_VALUE_HEADS, PAIR_WIDTH)
    d_k = apply_rotation(d_pairs[..., :HEAD_SIZE], cosine, -sine)
    d_gain_query = jnp.sum(d_q * q_unit, axis=(0, 1))
    d_gain_key = jnp.sum(d_k * k_unit, axis=(0, 1))
    d_q_raw = normalized_gradient(d_q * gain_query, q_unit, q_scale).reshape(tokens, QUERY_WIDTH)
    d_k_raw = normalized_gradient(d_k * gain_key, k_unit, k_scale)
    d_kv_raw = jnp.concatenate([d_k_raw, d_pairs[..., HEAD_SIZE:]], axis=-1).reshape(
        tokens, KV_WIDTH
    )
    d_qkv = jnp.concatenate([d_q_raw, d_kv_raw], axis=-1).astype(low)
    with jax.named_scope("grad_qkv"):
        qkv_term = contract_rows(normed, d_qkv).astype(low)
    with jax.named_scope("scatter_qkv"):
        qkv_sum = lax.psum_scatter(
            qkv_term.reshape(dp_count, D // dp_count, QUERY_WIDTH + KV_WIDTH),
            "seq", scatter_dimension=1, tiled=True,
        )
    with jax.named_scope("return_qkv"):
        qkv_own = reduce_blocks(qkv_sum)
    grad_qkv = jnp.concatenate(
        [qkv_own[:, :QUERY_WIDTH], unpaired(qkv_own[:, QUERY_WIDTH:])], axis=1
    )
    with jax.named_scope("back_qkv"):
        d_first = contract_cols(d_qkv, w_query)
    d_gain_one = jnp.sum(d_first * x_unit, axis=0)
    d_inputs = join(d_mixed) + normalized_gradient(d_first * gain_one, x_unit, x_scale)
    in_grad = d_inputs.astype(low).reshape(row_count, rows, D)

    with jax.named_scope("reduce_gains"):
        gain_term = jnp.concatenate([d_gain_one, d_gain_two, d_gain_query, d_gain_key])
        gain_term = gain_term.reshape(dp_count, seq_count, -1)
        for bit in orders[0]:
            gain_term = gain_term + crossed(gain_term, bit)
        grad_gains = lax.dynamic_index_in_dim(reduce_blocks(gain_term), place, 0, keepdims=False)
    return (
        block_out, in_grad, grad_qkv, grad_out, grad_gate_up, grad_down, grad_gains
    )


def solution(mesh):
    both = ("dp", "seq")
    return jax.shard_map(
        per_device,
        mesh=mesh,
        in_specs=(
            P("dp", "seq", None),
            P(both, None),
            P(both, None),
            P(both, None),
            P(both, None),
            P(both),
            P("dp", "seq"),
            P("dp", "seq"),
            P("dp", "seq", None),
        ),
        out_specs=(
            P("dp", "seq", None),
            P("dp", "seq", None),
            P(both, None),
            P(both, None),
            P(both, None),
            P(both, None),
            P(both),
        ),
        check_vma=False,
    )
```

time: 3430 us -> 1110 us (0.32)
  waiting for transfers between devices: 2860 us -> 541 us
  matrix products: 334 us -> 178 us
  starting transfers between devices: 0.88 us -> 75.4 us
  local copies, waits for them, and re-layouts: 67.5 us -> 111 us
  Pallas kernels: 0 us -> 37.8 us
    unnamed x12 -> x9, waiting for transfers between devices: 1430 us -> 0.86 us
    reduce_scatter x3, waiting for transfers between devices: 877 us -> 195 us  [the longest x1 114 us: per_device(): lax.psum_scatter(gate_term.reshape(dp_count, D // dp_count, 2 * ff_part),...]
    all_gather x5 -> x4, waiting for transfers between devices: 560 us -> 0.01 us  [the longest x1 0.01 us: per_device(): w_query = lax.all_gather(qkv_low, ('dp', 'seq'), axis=0, tiled=True)]
    ppermute x0 -> x57, waiting for transfers between devices: none -> 345 us  [the longest x42 297 us: shifted(): lax.ppermute(piece, 'dp', [(i, (i + shift) % count) for i in range(count)])]
    dot_general x74 -> x7, matrix products: 179 us -> 59 us  [matmul(): return jnp.dot(left, right, preferred_element_type=jnp.float32)]
    ppermute x0 -> x57, starting transfers between devices: none -> 74.7 us  [the longest x42 63 us: shifted(): lax.ppermute(piece, 'dp', [(i, (i + shift) % count) for i in range(count)])]
    dot_general x4, matrix products: 90.5 us -> 46.4 us  [contract_rows(): lax.dot_general(left, right, (((0,), (0,)), ((), ())), preferred_element_...]
    pallas_call x0 -> x4, Pallas kernels: none -> 37.8 us  [the longest x2 21.5 us: attend_back(): pl.pallas_call(functools.partial(attend_back_kernel, offsets), grid=(KEY_...]
  transfers between devices with their start and end apart: 10 -> 65, of which waited for: 8 -> 34; matrix products, arithmetic and copies ran while one was open for 8% -> 24% of each run, Pallas kernels for 0% -> 3%
where the time goes in v1:
time: 1110 us; the launch traced here: 1100 us
  waiting for transfers between devices  541 us (49%)
  matrix products  178 us (16%)
  local copies, waits for them, and re-layouts  111 us (10%)
  blocking collectives  92.5 us (8%)
  starting transfers between devices  75.4 us (7%)
  other arithmetic  47.9 us (4%)
  Pallas kernels  37.8 us (3%)
  between operations  15.8 us (1%)
    ppermute x42, waiting for transfers between devices, shifted(): lax.ppermute(piece, 'dp', [(i, (i + shift) % count) for i in range(count)])  297 us
    reduce_scatter x1, waiting for transfers between devices, per_device(): lax.psum_scatter(gate_term.reshape(dp_count, D // dp_count, 2 * ff_part),...  114 us
    unnamed x1, blocking collectives  92.5 us
    dot_general x7, matrix products, contract_cols(): lax.dot_general(left, right, (((1,), (1,)), ((), ())), preferred_element_...  72.1 us
    reduce_scatter x1, waiting for transfers between devices, per_device(): lax.psum_scatter(qkv_term.reshape(dp_count, D // dp_count, QUERY_WIDTH +...  70.1 us
    ppermute x42, starting transfers between devices, shifted(): lax.ppermute(piece, 'dp', [(i, (i + shift) % count) for i in range(count)])  63 us
    dot_general x7, matrix products, matmul(): return jnp.dot(left, right, preferred_element_type=jnp.float32)  59 us
    ppermute x15, waiting for transfers between devices, crossed(): return lax.ppermute(piece, 'seq', [(i, i ^ bit) for i in range(count)])  47.6 us
  transfers between devices with their start and end apart: 65, of which 34 were waited for; matrix products, arithmetic and copies ran while one was open for 24% of the time, Pallas kernels for 3%

profile of v1, /device:TPU:14, one launch (start us, length us, event | category | flops | bytes accessed | tf_op | source)
XLA Modules:
  0.0 1098.5 jit_solution(5866489651023500606)
XLA Ops:
  52.8 15.1 %collective-permute-done.9 = bf16[64,4096]{1,0:T(8,128)(2,1)S(1)} collective-permute-done((bf16[64,4096]{1,0:T(8,128)(2,1)}, bf16[64,4096]{1,0:T(8,128)(2,1)S(1)}, u32[]{:S(2)}, u32[]{:S(2)}) %collective-permute-start.9) | collective-permute-done | bytes 524320 | tf_op jit(solution)/shard_map/swap_gate/ppermute | solution.py:70
  67.9 21.4 %collective-permute-done.10 = bf16[64,4096]{1,0:T(8,128)(2,1)S(1)} collective-permute-done((bf16[64,4096]{1,0:T(8,128)(2,1)}, bf16[64,4096]{1,0:T(8,128)(2,1)S(1)}, u32[]{:S(2)}, u32[]{:S(2)}) %collective-permute-start.10) | collective-permute-done | bytes 524320 | tf_op jit(solution)/shard_map/swap_gate/ppermute | solution.py:70
  89.4 28.8 %collective-permute-done.11 = bf16[64,4096]{1,0:T(8,128)(2,1)} collective-permute-done((bf16[64,4096]{1,0:T(8,128)(2,1)}, bf16[64,4096]{1,0:T(8,128)(2,1)}, u32[]{:S(2)}, u32[]{:S(2)}) %collective-permute-start.11) | collective-permute-done | bytes 524320 | tf_op jit(solution)/shard_map/swap_gate/ppermute | solution.py:70
  134.8 92.5 %all-reduce = bf16[4224]{0:T(1024)(128)(2,1)S(1)} all-reduce(bf16[4224]{0:T(1024)(128)(2,1)S(1)} %dynamic-update-slice), channel_id=1, replica_groups=mesh['dp'=4,'seq'=8] {'dp','seq'}, use_global_device_ids=true, to_apply=%add | all-reduce | flops 4224 | bytes 16896
  273.7 13.6 %collective-permute-done.16 = bf16[256,640]{1,0:T(8,128)(2,1)S(1)} collective-permute-done((bf16[256,640]{1,0:T(8,128)(2,1)S(1)}, bf16[256,640]{1,0:T(8,128)(2,1)S(1)}, u32[]{:S(2)}, u32[]{:S(2)}) %collective-permute-start.16) | collective-permute-done | bytes 327712 | tf_op jit(solution)/shard_map/gather_kv1/ppermute | solution.py:125
  322.1 30.1 %collective-permute-done.6 = bf16[128,2048]{1,0:T(8,128)(2,1)} collective-permute-done((bf16[128,2048]{1,0:T(8,128)(2,1)}, bf16[128,2048]{1,0:T(8,128)(2,1)}, u32[]{:S(2)}, u32[]{:S(2)}) %collective-permute-start.6) | collective-permute-done | bytes 524320 | tf_op jit(solution)/shard_map/swap_normed0/ppermute | solution.py:70
  383.8 29.3 %collective-permute-done.19 = bf16[128,2048]{1,0:T(8,128)(2,1)S(1)} collective-permute-done((bf16[128,2048]{1,0:T(8,128)(2,1)S(1)}, bf16[128,2048]{1,0:T(8,128)(2,1)S(1)}, u32[]{:S(2)}, u32[]{:S(2)}) %collective-permute-start.19) | collective-permute-done | bytes 524320 | tf_op jit(solution)/shard_map/swap_normed1/ppermute | solution.py:70
  417.7 14.4 %fusion.34 = f32[512,4096]{1,0:T(8,128)} fusion(bf16[2048,4096]{1,0:T(8,128)(2,1)} %bitcast.212, bf16[128,2048]{1,0:T(8,128)(2,1)S(1)} %collective-permute-done.20, bf16[128,2048]{1,0:T(8,128)(2,1)S(1)} %collective-permute-done.19, bf16[128,2048]{1,0:T(8,128)(2,1)S(1)} %collective-permute-done.18, bf16[128,2048]{1,0:T(8,128)(2,1)S(1)} %get-tuple-element.44), kind=kOutput, calls=%fused_computation.49 | convolution fusion | flops 8598323200 | bytes 27262976 | tf_op jit(solution)/shard_map/gate_up1/dot_general | solution.py:53
  432.2 13.1 %multiply_convert_fusion.1 = (bf16[512,2048]{1,0:T(8,128)(2,1)}, bf16[512,2048]{1,0:T(8,128)(2,1)}, bf16[512,2048]{1,0:T(8,128)(2,1)S(1)}) fusion(f32[512,4096]{1,0:T(8,128)} %fusion.34, bf16[2048,2048]{1,0:T(8,128)(2,1)} %all-gather.11.cloned.1.call-done, bf16[128,2048]{1,0:T(8,128)(2,1)S(1)} %collective-permute-done.29, ...), kind=kOutput, calls=%fused_computation.24 | convolution fusion | flops 4319084544 | bytes 25165824 | tf_op jit(solution)/shard_map/back_down1/dot_general | solution.py:63
  445.3 14.4 %fusion.20 = bf16[512,2048]{1,0:T(8,128)(2,1)S(1)} fusion(bf16[2048,4096]{1,0:T(8,128)(2,1)} %bitcast.213, bf16[512,2048]{1,0:T(8,128)(2,1)} %get-tuple-element.50, bf16[512,2048]{1,0:T(8,128)(2,1)} %get-tuple-element.49), kind=kOutput, calls=%fused_computation.33 | convolution fusion | flops 8599371776 | bytes 23068672 | tf_op jit(solution)/shard_map/back_gate1/dot_general | solution.py:63
  464.4 15.0 %fusion.26 = f32[512,4096]{1,0:T(8,128)} fusion(bf16[2048,4096]{1,0:T(8,128)(2,1)} %bitcast.214, bf16[128,2048]{1,0:T(8,128)(2,1)} %collective-permute-done.8, bf16[128,2048]{1,0:T(8,128)(2,1)} %collective-permute-done.7, bf16[128,2048]{1,0:T(8,128)(2,1)} %collective-permute-done.6, bf16[128,2048]{1,0:T(8,128)(2,1)} %get-tuple-element.46), kind=kOutput, calls=%fused_computation.41 | convolution fusion | flops 8598323200 | bytes 27262976 | tf_op jit(solution)/shard_map/gate_up0/dot_general | solution.py:53
  479.3 13.4 %multiply_convert_fusion.3 = (bf16[512,2048]{1,0:T(8,128)(2,1)}, bf16[512,2048]{1,0:T(8,128)(2,1)}, bf16[512,2048]{1,0:T(8,128)(2,1)}) fusion(f32[512,4096]{1,0:T(8,128)} %fusion.26, bf16[2048,2048]{1,0:T(8,128)(2,1)} %all-gather.11.cloned.1.call-done, bf16[128,2048]{1,0:T(8,128)(2,1)} %collective-permute-done.26, ...), kind=kOutput, calls=%fused_computation.26 | convolution fusion | flops 4319084544 | bytes 25165824 | tf_op jit(solution)/shard_map/back_down0/dot_general | solution.py:63
  492.7 13.7 %fusion.23 = bf16[512,2048]{1,0:T(8,128)(2,1)S(1)} fusion(bf16[2048,4096]{1,0:T(8,128)(2,1)} %bitcast.215, bf16[512,2048]{1,0:T(8,128)(2,1)} %get-tuple-element.48, bf16[512,2048]{1,0:T(8,128)(2,1)} %get-tuple-element.47), kind=kOutput, calls=%fused_computation.34 | convolution fusion | flops 8599371776 | bytes 23068672 | tf_op jit(solution)/shard_map/back_gate0/dot_general | solution.py:63
  510.7 24.9 %convolution_convert_fusion = bf16[2048,4096]{1,0:T(8,128)(2,1)} fusion(bf16[1024,2048]{1,0:T(8,128)(2,1)} %constant_dynamic-update-slice_fusion, bf16[512,2048]{1,0:T(8,128)(2,1)} %get-tuple-element.50, bf16[512,2048]{1,0:T(8,128)(2,1)} %get-tuple-element.49, bf16[512,2048]{1,0:T(8,128)(2,1)} %get-tuple-element.48, bf16[512,2048]{1,0:T(8,128)(2,1)} %get-tuple-element.47), kind=kOutput, calls=%fused_computation | convolution fusion | flops 17221812224 | bytes 29360128 | tf_op jit(solution)/shard_map/grad_gate/dot_general | solution.py:57
  535.6 13.4 %convolution_convert_fusion.2 = bf16[2048,2048]{1,0:T(8,128)(2,1)} fusion(bf16[1024,2048]{1,0:T(8,128)(2,1)} %constant_dynamic-update-slice_fusion.8, bf16[512,2048]{1,0:T(8,128)(2,1)S(1)} %get-tuple-element.52, bf16[512,2048]{1,0:T(8,128)(2,1)S(1)} %copy-done.61), kind=kOutput, calls=%fused_computation.9 | convolution fusion | flops 8602517504 | bytes 16777216 | tf_op jit(solution)/shard_map/grad_down/dot_general | solution.py:57
  575.1 29.4 %collective-permute-done.32 = bf16[128,2048]{1,0:T(8,128)(2,1)S(1)} collective-permute-done((bf16[128,2048]{1,0:T(8,128)(2,1)S(1)}, bf16[128,2048]{1,0:T(8,128)(2,1)S(1)}, u32[]{:S(2)}, u32[]{:S(2)}) %collective-permute-start.32) | collective-permute-done | bytes 524320 | tf_op jit(solution)/shard_map/reduce_normed0/ppermute | solution.py:70
  610.2 28.1 %collective-permute-done.13 = bf16[128,2048]{1,0:T(8,128)(2,1)S(1)} collective-permute-done((bf16[128,2048]{1,0:T(8,128)(2,1)S(1)}, bf16[128,2048]{1,0:T(8,128)(2,1)S(1)}, u32[]{:S(2)}, u32[]{:S(2)}) %collective-permute-start.13) | collective-permute-done | bytes 524320 | tf_op jit(solution)/shard_map/reduce_down0/ppermute | solution.py:70
  638.3 11.2 %collective-permute-done.14 = bf16[128,2048]{1,0:T(8,128)(2,1)S(1)} collective-permute-done((bf16[128,2048]{1,0:T(8,128)(2,1)S(1)}, bf16[128,2048]{1,0:T(8,128)(2,1)S(1)}, u32[]{:S(2)}, u32[]{:S(2)}) %collective-permute-start.14) | collective-permute-done | bytes 524320 | tf_op jit(solution)/shard_map/reduce_down0/ppermute | solution.py:70
  694.0 10.7 attend_back0.1
  709.8 10.8 attend_back1.1
  813.8 10.9 reduce-scatter.11.cloned.1.call-done
  827.4 70.1 %reduce-scatter.7.cloned.1.call-done = bf16[4,64,1920]{2,1,0:T(8,128)(2,1)} async-done(((bf16[4,512,1920]{2,1,0:T(8,128)(2,1)}), bf16[4,64,1920]{2,1,0:T(8,128)(2,1)}) %reduce-scatter.7.cloned.1.call-update) | async-done | bytes 983056 | tf_op jit(solution)/shard_map/scatter_qkv/reduce_scatter | solution.py:472
  903.3 114.0 %reduce-scatter.9.cloned.1.call-done = bf16[4,64,4096]{2,1,0:T(8,128)(2,1)} async-done(((bf16[4,512,4096]{2,1,0:T(8,128)(2,1)}), bf16[4,64,4096]{2,1,0:T(8,128)(2,1)}) %reduce-scatter.9.cloned.1.call-update) | async-done | bytes 2097168 | tf_op jit(solution)/shard_map/scatter_gate/reduce_scatter | solution.py:409
  1027.0 29.2 %collective-permute-done.48 = bf16[64,4096]{1,0:T(8,128)(2,1)S(1)} collective-permute-done((bf16[64,4096]{1,0:T(8,128)(2,1)S(1)}, bf16[64,4096]{1,0:T(8,128)(2,1)S(1)}, u32[]{:S(2)}, u32[]{:S(2)}) %collective-permute-start.48) | collective-permute-done | bytes 524320 | tf_op jit(solution)/shard_map/return_gate/ppermute | solution.py:70
  (437 shorter events, 415.1 us)
Async XLA Ops:
  7.2 230.7 %all-gather.5.cloned.1.call-start = ((), (), s32[]{:S(2)}) async-start(), calls=%async_computation.4 | async-start | bytes 8110080 | tf_op jit(solution)/shard_map/gather_qkv/all_gather | solution.py:307
  10.6 288.2 %all-gather.7.cloned.1.call-start = ((), (), s32[]{:S(2)}) async-start(), calls=%async_computation.5 | async-start | bytes 5898240 | tf_op jit(solution)/shard_map/gather_out/all_gather | solution.py:324
  33.7 384.0 %all-gather.9.cloned.1.call-start = ((), (), s32[]{:S(2)}) async-start(), calls=%async_computation.6 | async-start | bytes 18874368 | tf_op jit(solution)/shard_map/gather_gate/all_gather | solution.py:326
  52.8 65.3 %collective-permute-start.11 = (bf16[64,4096]{1,0:T(8,128)(2,1)}, bf16[64,4096]{1,0:T(8,128)(2,1)}, u32[]{:S(2)}, u32[]{:S(2)}) collective-permute-start(bf16[64,4096]{1,0:T(8,128)(2,1)} %get-tuple-element.70), channel_id=1, source_target_pairs={{0,8},{8,16},{16,24},{24,0},{1,9},{9,17},{17,25},{25,1},{2,10},{10... | collective-permute-start | bytes 1572872 | tf_op jit(solution)/shard_map/swap_gate/ppermute | solution.py:70
  122.2 310.0 %all-gather.11.cloned.1.call-start = ((), (), s32[]{:S(2)}) async-start(), calls=%async_computation.7 | async-start | bytes 9437184 | tf_op jit(solution)/shard_map/gather_down/all_gather | solution.py:328
  123.3 244.9 %collective-permute-start.27 = (bf16[128,2048]{1,0:T(8,128)(2,1)}, bf16[128,2048]{1,0:T(8,128)(2,1)}, u32[]{:S(2)}, u32[]{:S(2)}) collective-permute-start(bf16[128,2048]{1,0:T(8,128)(2,1)} %get-tuple-element.84), channel_id=1, source_target_pairs={{0,8},{8,16},{16,24},{24,0},{1,9},{9,17},{17,25},{25,1},{2,10},{10... | collective-permute-start | bytes 1572872 | tf_op jit(solution)/shard_map/swap_grad/ppermute | solution.py:70
  125.7 247.8 %collective-permute-start.28 = (bf16[128,2048]{1,0:T(8,128)(2,1)}, bf16[128,2048]{1,0:T(8,128)(2,1)}, u32[]{:S(2)}, u32[]{:S(2)}) collective-permute-start(bf16[128,2048]{1,0:T(8,128)(2,1)} %get-tuple-element.84), channel_id=1, source_target_pairs={{0,16},{8,24},{16,0},{24,8},{1,17},{9,25},{17,1},{25,9},{2,18},{10... | collective-permute-start | bytes 1572872 | tf_op jit(solution)/shard_map/swap_grad/ppermute | solution.py:70
  129.5 102.6 %collective-permute-start.24 = (bf16[128,2048]{1,0:T(8,128)(2,1)}, bf16[128,2048]{1,0:T(8,128)(2,1)}, u32[]{:S(2)}, u32[]{:S(2)}) collective-permute-start(bf16[128,2048]{1,0:T(8,128)(2,1)} %get-tuple-element.83), channel_id=1, source_target_pairs={{0,8},{8,16},{16,24},{24,0},{1,9},{9,17},{17,25},{25,1},{2,10},{10... | collective-permute-start | bytes 1572872 | tf_op jit(solution)/shard_map/swap_grad/ppermute | solution.py:70
  129.6 104.5 %collective-permute-start.25 = (bf16[128,2048]{1,0:T(8,128)(2,1)}, bf16[128,2048]{1,0:T(8,128)(2,1)}, u32[]{:S(2)}, u32[]{:S(2)}) collective-permute-start(bf16[128,2048]{1,0:T(8,128)(2,1)} %get-tuple-element.83), channel_id=1, source_target_pairs={{0,16},{8,24},{16,0},{24,8},{1,17},{9,25},{17,1},{25,9},{2,18},{10... | collective-permute-start | bytes 1572872 | tf_op jit(solution)/shard_map/swap_grad/ppermute | solution.py:70
  129.6 106.4 %collective-permute-start.26 = (bf16[128,2048]{1,0:T(8,128)(2,1)}, bf16[128,2048]{1,0:T(8,128)(2,1)}, u32[]{:S(2)}, u32[]{:S(2)}) collective-permute-start(bf16[128,2048]{1,0:T(8,128)(2,1)} %get-tuple-element.83), channel_id=1, source_target_pairs={{0,24},{8,0},{16,8},{24,16},{1,25},{9,1},{17,9},{25,17},{2,26},{10... | collective-permute-start | bytes 1572872 | tf_op jit(solution)/shard_map/swap_grad/ppermute | solution.py:70
  134.5 656.3 %reduce-scatter.13.cloned.1.call-start = ((), (), s32[]{:S(2)}) async-start(), calls=%async_computation.11 | async-start | bytes 5898240
  460.9 105.3 %collective-permute-start.33 = (bf16[128,2048]{1,0:T(8,128)(2,1)}, bf16[128,2048]{1,0:T(8,128)(2,1)S(1)}, u32[]{:S(2)}, u32[]{:S(2)}) collective-permute-start(bf16[128,2048]{1,0:T(8,128)(2,1)} %get-tuple-element.58), channel_id=1, source_target_pairs={{0,24},{8,0},{16,8},{24,16},{1,25},{9,1},{17,9},{25,17},{2,26},{10... | collective-permute-start | bytes 1572872 | tf_op jit(solution)/shard_map/reduce_normed1/ppermute | solution.py:70
  461.0 108.8 %collective-permute-start.34 = (bf16[128,2048]{1,0:T(8,128)(2,1)}, bf16[128,2048]{1,0:T(8,128)(2,1)S(1)}, u32[]{:S(2)}, u32[]{:S(2)}) collective-permute-start(bf16[128,2048]{1,0:T(8,128)(2,1)} %get-tuple-element.60), channel_id=1, source_target_pairs={{0,16},{8,24},{16,0},{24,8},{1,17},{9,25},{17,1},{25,9},{2,18},{10... | collective-permute-start | bytes 1572872 | tf_op jit(solution)/shard_map/reduce_normed1/ppermute | solution.py:70
  462.0 107.8 %collective-permute-start.35 = (bf16[128,2048]{1,0:T(8,128)(2,1)}, bf16[128,2048]{1,0:T(8,128)(2,1)}, u32[]{:S(2)}, u32[]{:S(2)}) collective-permute-start(bf16[128,2048]{1,0:T(8,128)(2,1)} %get-tuple-element.59), channel_id=1, source_target_pairs={{0,8},{8,16},{16,24},{24,0},{1,9},{9,17},{17,25},{25,1},{2,10},{10... | collective-permute-start | bytes 1572872 | tf_op jit(solution)/shard_map/reduce_normed1/ppermute | solution.py:70
  508.3 66.9 %collective-permute-start.31 = (bf16[128,2048]{1,0:T(8,128)(2,1)}, bf16[128,2048]{1,0:T(8,128)(2,1)}, u32[]{:S(2)}, u32[]{:S(2)}) collective-permute-start(bf16[128,2048]{1,0:T(8,128)(2,1)} %get-tuple-element.63), channel_id=1, source_target_pairs={{0,16},{8,24},{16,0},{24,8},{1,17},{9,25},{17,1},{25,9},{2,18},{10... | collective-permute-start | bytes 1572872 | tf_op jit(solution)/shard_map/reduce_normed0/ppermute | solution.py:70
  569.8 68.5 %collective-permute-start.13 = (bf16[128,2048]{1,0:T(8,128)(2,1)S(1)}, bf16[128,2048]{1,0:T(8,128)(2,1)S(1)}, u32[]{:S(2)}, u32[]{:S(2)}) collective-permute-start(bf16[128,2048]{1,0:T(8,128)(2,1)S(1)} %get-tuple-element.66), channel_id=1, source_target_pairs={{0,16},{8,24},{16,0},{24,8},{1,17},{9,25},{17,1},{25,9},{2,18},{10... | collective-permute-start | bytes 1572872 | tf_op jit(solution)/shard_map/reduce_down0/ppermute | solution.py:70
  572.6 76.9 %collective-permute-start.14 = (bf16[128,2048]{1,0:T(8,128)(2,1)S(1)}, bf16[128,2048]{1,0:T(8,128)(2,1)S(1)}, u32[]{:S(2)}, u32[]{:S(2)}) collective-permute-start(bf16[128,2048]{1,0:T(8,128)(2,1)S(1)} %get-tuple-element.65), channel_id=1, source_target_pairs={{0,8},{8,16},{16,24},{24,0},{1,9},{9,17},{17,25},{25,1},{2,10},{10... | collective-permute-start | bytes 1572872 | tf_op jit(solution)/shard_map/reduce_down0/ppermute | solution.py:70
  575.1 85.1 %collective-permute-start.21 = (bf16[128,2048]{1,0:T(8,128)(2,1)S(1)}, bf16[128,2048]{1,0:T(8,128)(2,1)S(1)}, u32[]{:S(2)}, u32[]{:S(2)}) collective-permute-start(bf16[128,2048]{1,0:T(8,128)(2,1)S(1)} %get-tuple-element.67), channel_id=1, source_target_pairs={{0,24},{8,0},{16,8},{24,16},{1,25},{9,1},{17,9},{25,17},{2,26},{10... | collective-permute-start | bytes 1572872 | tf_op jit(solution)/shard_map/reduce_down1/ppermute | solution.py:70
  686.6 138.0 %reduce-scatter.11.cloned.1.call-start = ((), (), s32[]{:S(2)}) async-start(), calls=%async_computation.10 | async-start | bytes 9437184 | tf_op jit(solution)/shard_map/scatter_down/reduce_scatter | solution.py:414
  687.2 210.4 %reduce-scatter.7.cloned.1.call-start = ((), (), s32[]{:S(2)}) async-start(), calls=%async_computation.8 | async-start | bytes 8847360 | tf_op jit(solution)/shard_map/scatter_qkv/reduce_scatter | solution.py:472
  767.7 249.7 %reduce-scatter.9.cloned.1.call-start = ((), (), s32[]{:S(2)}) async-start(), calls=%async_computation.9 | async-start | bytes 18874368 | tf_op jit(solution)/shard_map/scatter_gate/reduce_scatter | solution.py:409
  898.8 120.6 %collective-permute-start.42 = (bf16[64,1920]{1,0:T(8,128)(2,1)S(1)}, bf16[64,1920]{1,0:T(8,128)(2,1)S(1)}, u32[]{:S(2)}, u32[]{:S(2)}) collective-permute-start(bf16[64,1920]{1,0:T(8,128)(2,1)S(1)} %get-tuple-element.85), channel_id=1, source_target_pairs={{0,8},{8,16},{16,24},{24,0},{1,9},{9,17},{17,25},{25,1},{2,10},{10... | collective-permute-start | bytes 737288 | tf_op jit(solution)/shard_map/return_qkv/ppermute | solution.py:70
  900.4 119.0 %collective-permute-start.43 = (bf16[64,1920]{1,0:T(8,128)(2,1)S(1)}, bf16[64,1920]{1,0:T(8,128)(2,1)S(1)}, u32[]{:S(2)}, u32[]{:S(2)}) collective-permute-start(bf16[64,1920]{1,0:T(8,128)(2,1)S(1)} %get-tuple-element.87), channel_id=1, source_target_pairs={{0,16},{8,24},{16,0},{24,8},{1,17},{9,25},{17,1},{25,9},{2,18},{10... | collective-permute-start | bytes 737288 | tf_op jit(solution)/shard_map/return_qkv/ppermute | solution.py:70
  901.8 117.7 %collective-permute-start.44 = (bf16[64,1920]{1,0:T(8,128)(2,1)S(1)}, bf16[64,1920]{1,0:T(8,128)(2,1)}, u32[]{:S(2)}, u32[]{:S(2)}) collective-permute-start(bf16[64,1920]{1,0:T(8,128)(2,1)S(1)} %get-tuple-element.86), channel_id=1, source_target_pairs={{0,24},{8,0},{16,8},{24,16},{1,25},{9,1},{17,9},{25,17},{2,26},{10... | collective-permute-start | bytes 737288 | tf_op jit(solution)/shard_map/return_qkv/ppermute | solution.py:70
  (104 other events, 2293.1 us)
Sparse Core Ops, SparseCore 0:
  11.5 108.1 all-gather.4
  121.5 42.0 all-gather.6
  166.2 92.0 all-gather.8
  260.6 61.1 all-gather.10
  686.7 62.2 reduce-scatter.12
  752.4 72.2 reduce-scatter.10
  828.1 69.4 reduce-scatter.6
  901.1 116.1 reduce-scatter.8

commit v2 on v1

v2 whole, which is shorter than its diff:
```python
import functools

import jax
import jax.numpy as jnp
from jax import lax
from jax.experimental import pallas as pl
from jax.experimental.pallas import tpu as pltpu
from jax.sharding import PartitionSpec as P


D = 2048
QUERY_HEADS = 20
KEY_VALUE_HEADS = 5
HEAD_SIZE = 64
FF = 8192
GROUP = QUERY_HEADS // KEY_VALUE_HEADS
QUERY_WIDTH = QUERY_HEADS * HEAD_SIZE
PAIR_WIDTH = 2 * HEAD_SIZE
KV_WIDTH = KEY_VALUE_HEADS * PAIR_WIDTH
GROUP_WIDTH = GROUP * HEAD_SIZE

EPSILON = 1e-06
MASKED = -1e30
SCALE = HEAD_SIZE ** (-0.5)


def normalized_rows(values):
    scale_rows = lax.rsqrt(jnp.mean(values * values, axis=-1, keepdims=True) + EPSILON)
    return (values * scale_rows, scale_rows)


def normalized_gradient(upstream, unit_vals, scale_rows):
    return scale_rows * (
        upstream - unit_vals * jnp.mean(upstream * unit_vals, axis=-1, keepdims=True)
    )


def rope_tables(positions):
    freq = 1.0 / 10000.0 ** (jnp.arange(0, HEAD_SIZE, 2).astype(jnp.float32) / HEAD_SIZE)
    angle = positions.astype(jnp.float32)[:, None, :] * freq[None, :, None]
    return jnp.stack([jnp.cos(angle), jnp.sin(angle)], axis=1)


def matmul(left, right):
    return jnp.dot(left, right, preferred_element_type=jnp.float32)


def contract_rows(left, right):
    return lax.dot_general(
        left, right, (((0,), (0,)), ((), ())), preferred_element_type=jnp.float32
    )


def contract_cols(left, right):
    return lax.dot_general(
        left, right, (((1,), (1,)), ((), ())), preferred_element_type=jnp.float32
    )


def shifted(piece, shift):
    count = lax.axis_size("dp")
    return lax.ppermute(piece, "dp", [(i, (i + shift) % count) for i in range(count)])


def rotate_gather(piece):
    return [piece] + [shifted(piece, s) for s in range(1, lax.axis_size("dp"))]


def line_gather(piece):
    count = lax.axis_size("dp")
    me = lax.axis_index("dp")
    up, down, ups, downs = piece, piece, [], []
    for hop in range(1, count):
        up = lax.ppermute(up, "dp", [(i, i + 1) for i in range(hop - 1, count - 1)])
        down = lax.ppermute(down, "dp", [(i, i - 1) for i in range(1, count + 1 - hop)])
        ups.append(up)
        downs.append(down)
    return [piece] + [
        jnp.where(me >= s, ups[s - 1], downs[count - s - 1]) for s in range(1, count)
    ]


def rotate_slots(partial, rows):
    return [partial[:rows]] + [
        shifted(partial[s * rows : (s + 1) * rows].astype(jnp.bfloat16), -s)
        for s in range(1, lax.axis_size("dp"))
    ]


def line_reduce(partial, rows):
    count = lax.axis_size("dp")
    slots = [partial[s * rows : (s + 1) * rows] for s in range(count)]
    up, down = slots[1], slots[count - 1]
    for hop in range(1, count):
        if hop > 1:
            up = (slots[hop].astype(jnp.float32) + up.astype(jnp.float32)).astype(jnp.bfloat16)
            down = (slots[count - hop].astype(jnp.float32) + down.astype(jnp.float32)).astype(
                jnp.bfloat16
            )
        up = lax.ppermute(up, "dp", [(i, i + 1) for i in range(hop)])
        down = lax.ppermute(down, "dp", [(i, i - 1) for i in range(count - hop, count)])
    return added([slots[0], up, down])


def added(slots):
    return functools.reduce(jnp.add, [slot.astype(jnp.float32) for slot in slots])


def in_order(slots):
    count = len(slots)
    back = slots[::-1] + slots[::-1]
    start = count - 1 - lax.axis_index("dp")
    return lax.dynamic_slice_in_dim(jnp.stack(back[:-1]), start, count, axis=0)


def exchange_blocks(pick):
    count = lax.axis_size("dp")
    me = lax.axis_index("dp")
    return in_order([pick(me)] + [shifted(pick(lax.rem(me + s, count)), s) for s in range(1, count)])


def reduce_blocks(blocks):
    count = lax.axis_size("dp")
    me = lax.axis_index("dp")
    pick = lambda s: lax.dynamic_index_in_dim(blocks, lax.rem(me + s, count), 0, keepdims=False)
    total = pick(0).astype(jnp.float32)
    for s in range(1, count):
        total = total + shifted(pick(s), s).astype(jnp.float32)
    return total


def bit_orders(count, ways):
    bits = [1 << i for i in range(1, count.bit_length() - 1)]
    half = (len(bits) + 1) // 2
    low, high = bits[:half], bits[half:]
    orders = []
    for way in range(ways):
        one, two = (low, high) if way % 2 == 0 else (high, low)
        order = []
        for i in range(half):
            order += one[i : i + 1] + two[i : i + 1]
        orders.append(tuple(order + [1]))
    return orders


def crossed(piece, bit):
    count = lax.axis_size("seq")
    return lax.ppermute(piece, "seq", [(i, i ^ bit) for i in range(count)])


def cube_gather(piece, bits):
    for bit in bits:
        other = crossed(piece, bit)
        piece = jnp.concatenate([piece, other], axis=0)
    return piece


def cube_gather_in_order(piece):
    bit = 1
    while bit < lax.axis_size("seq"):
        other = crossed(piece, bit)
        upper = (lax.axis_index("seq") & bit) > 0
        piece = jnp.where(
            upper, jnp.concatenate([other, piece]), jnp.concatenate([piece, other])
        )
        bit *= 2
    return piece


def cube_offsets(bits):
    offsets = [0]
    for bit in bits:
        offsets = offsets + [o ^ bit for o in offsets]
    return tuple(offsets)


def cube_reduce(partial, bits):
    for bit in bits[::-1]:
        half = partial.shape[0] // 2
        other = crossed(partial[half:].astype(jnp.bfloat16), bit)
        partial = partial[:half].astype(jnp.float32) + other.astype(jnp.float32)
    return partial


def cube_scatter(term, bits):
    me = lax.axis_index("seq")
    left = sorted(bits)
    for bit in bits[::-1]:
        low_count = 1 << left.index(bit)
        left.remove(bit)
        lead, _, *rest = term.shape
        view = term.reshape(lead, -1, 2, low_count, *rest)
        mine = jnp.minimum(me & bit, 1)
        pick = lambda i: lax.dynamic_index_in_dim(view, i, 2, keepdims=False).reshape(
            lead, -1, *rest
        )
        other = crossed(pick(1 - mine).astype(jnp.bfloat16), bit)
        term = pick(mine).astype(jnp.float32) + other.astype(jnp.float32)
    return term[:, 0]


def halves_scatter(term, orders):
    half = term.shape[0] // 2
    return jnp.concatenate(
        [cube_scatter(term[:half], orders[0]), cube_scatter(term[half:], orders[1])]
    ).astype(jnp.bfloat16)


def fill_bias(place_ref, start_ref, bias_ref, offsets):
    rows = start_ref.shape[1]
    place = place_ref[0]
    query = place * rows + lax.broadcasted_iota(jnp.int32, (rows, rows), 1)
    begin = start_ref[...]
    local = lax.broadcasted_iota(jnp.int32, (rows, rows), 0)
    for slot, offset in enumerate(offsets):
        key = (place ^ offset) * rows + local
        allowed = (key <= query) & (key >= begin)
        bias_ref[slot * rows : (slot + 1) * rows, :] = jnp.where(allowed, 0.0, MASKED)


def unstacked_heads(turned):
    rows = turned.shape[1] // GROUP
    return jnp.concatenate([turned[:, g * rows : (g + 1) * rows] for g in range(GROUP)], axis=0).T


def each_row(offsets, place_ref, start_ref, bias_ref):
    for r, order in enumerate(offsets):

        @pl.when((pl.program_id(0) == r) & (pl.program_id(1) == 0))
        def _():
            fill_bias(place_ref, start_ref, bias_ref, order)


def side_by_side(block):
    turned = block.astype(jnp.float32).T
    return jnp.concatenate(
        [turned[g * HEAD_SIZE : (g + 1) * HEAD_SIZE] for g in range(GROUP)], axis=1
    )


def unit_columns(values):
    scale = lax.rsqrt(jnp.mean(values * values, axis=0, keepdims=True) + EPSILON)
    return values * scale, scale


def turn_columns(values, cosine, sine):
    half = HEAD_SIZE // 2
    first, second = values[:half], values[half:]
    return jnp.concatenate(
        [first * cosine - second * sine, second * cosine + first * sine], axis=0
    )


def raw_gradient(upstream, unit, scale, gain, cosine, sine):
    straight = turn_columns(upstream, cosine, -sine)
    gained = straight * gain
    center = jnp.mean(gained * unit, axis=0, keepdims=True)
    return scale * (gained - unit * center), straight * unit


def prepared(block, gain, tables, heads):
    cosine = jnp.concatenate([tables[0]] * heads, axis=1)
    sine = jnp.concatenate([tables[1]] * heads, axis=1)
    unit, scale = unit_columns(block)
    return unit, scale, cosine, sine, turn_columns(unit * gain, cosine, sine)


def padded(heads, place):
    empty = jnp.zeros(heads.shape, jnp.bfloat16)
    return jnp.concatenate([heads, empty] if place == 0 else [empty, heads], axis=0)


def rounded_queries(turned):
    return padded((turned.astype(jnp.bfloat16).astype(jnp.float32) * SCALE).astype(jnp.bfloat16), 0)


def attend_kernel(
    offsets, place_ref, start_ref, gain_ref, table_ref, q_ref, kv_ref, out_ref, lse_ref, bias_ref
):
    each_row(offsets, place_ref, start_ref.at[0], bias_ref)
    pairs = kv_ref[...]
    block = side_by_side(q_ref[...])
    queries = rounded_queries(prepared(block, gain_ref[...], table_ref[0], GROUP)[-1])
    bias = jnp.concatenate([bias_ref[...]] * GROUP, axis=1)
    scores = matmul(pairs, queries) + bias
    peak = jnp.max(scores, axis=0, keepdims=True)
    raised = jnp.exp(scores - peak)
    totals = jnp.sum(raised, axis=0, keepdims=True)
    probs = (raised * (1.0 / totals)).astype(jnp.bfloat16)
    mixed = contract_rows(pairs, probs)
    out_ref[...] = unstacked_heads(mixed[HEAD_SIZE:]).astype(jnp.bfloat16)
    lse_ref[0, 0] = peak + jnp.log(totals)


def attend_back_kernel(
    offsets, place_ref, start_ref, gain_ref, table_ref, q_ref, kv_ref, do_ref, lse_ref,
    dq_ref, dkv_ref, dgain_ref, bias_ref,
):
    each_row(offsets, place_ref, start_ref.at[0], bias_ref)
    pairs = kv_ref[...]
    gain = gain_ref[...]
    unit, scale, cosine, sine, turned = prepared(
        side_by_side(q_ref[...]), gain, table_ref[0], GROUP
    )
    queries = rounded_queries(turned)
    upstream = padded(side_by_side(do_ref[...]).astype(jnp.bfloat16), 1)
    bias = jnp.concatenate([bias_ref[...]] * GROUP, axis=1)
    probs = jnp.exp(matmul(pairs, queries) + bias - lse_ref[0, 0])
    d_probs = matmul(pairs, upstream)
    center = jnp.sum(probs * d_probs, axis=0, keepdims=True)
    d_scores = (probs * (d_probs - center)).astype(jnp.bfloat16)
    d_pairs = contract_cols(d_scores, queries) + contract_cols(
        probs.astype(jnp.bfloat16), upstream
    )
    dkv_ref[...] = d_pairs.astype(jnp.bfloat16)
    d_queries = contract_rows(pairs, d_scores)[:HEAD_SIZE] * SCALE
    d_raw, d_gain = raw_gradient(d_queries, unit, scale, gain, cosine, sine)
    dq_ref[...] = unstacked_heads(d_raw).astype(jnp.bfloat16)

    @pl.when((pl.program_id(0) == 0) & (pl.program_id(1) == 0))
    def _():
        dgain_ref[...] = jnp.zeros_like(dgain_ref)

    rows = dgain_ref.shape[1]
    for g in range(GROUP):
        dgain_ref[...] += d_gain[:, g * rows : (g + 1) * rows]


def keys_kernel(gain_ref, table_ref, kv_ref, out_ref):
    turned = kv_ref[...].T
    keys = prepared(turned[:HEAD_SIZE], gain_ref[...], table_ref, 1)[-1]
    out_ref[...] = jnp.concatenate([keys, turned[HEAD_SIZE:]], axis=0).T.astype(jnp.bfloat16)


def keys_back_kernel(gain_ref, table_ref, kv_ref, d_ref, out_ref, dgain_ref):
    gain = gain_ref[...]
    unit, scale, cosine, sine, _ = prepared(kv_ref[...].T[:HEAD_SIZE], gain, table_ref, 1)
    upstream = d_ref[...].T
    d_raw, d_gain = raw_gradient(upstream[:HEAD_SIZE], unit, scale, gain, cosine, sine)
    out_ref[...] = jnp.concatenate([d_raw, upstream[HEAD_SIZE:]], axis=0).T.astype(jnp.bfloat16)

    @pl.when(pl.program_id(0) == 0)
    def _():
        dgain_ref[...] = jnp.zeros_like(dgain_ref)

    dgain_ref[...] += d_gain


def row_specs(rows, keys):
    whole = lambda shape: pl.BlockSpec(shape, lambda r, h: (0,) * len(shape))
    return (
        pl.BlockSpec(memory_space=pltpu.SMEM),
        pl.BlockSpec((1, 1, rows), lambda r, h: (r, 0, 0)),
        whole((HEAD_SIZE, 1)),
        pl.BlockSpec((1, 2, HEAD_SIZE // 2, rows), lambda r, h: (r, 0, 0, 0)),
        pl.BlockSpec((rows, GROUP_WIDTH), lambda r, h: (r, h)),
        pl.BlockSpec((keys, PAIR_WIDTH), lambda r, h: (r, h)),
        pl.BlockSpec((1, 1, 1, GROUP * rows), lambda r, h: (r, h, 0, 0)),
        whole((HEAD_SIZE, rows)),
    )


def attend(offsets, place, start, gain, tables, qkv, pairs):
    count = len(offsets)
    rows, keys = qkv.shape[0] // count, pairs.shape[0] // count
    at, begin, gains, turns, heads, blocks, lse, _ = row_specs(rows, keys)
    return pl.pallas_call(
        functools.partial(attend_kernel, offsets),
        grid=(count, KEY_VALUE_HEADS),
        in_specs=[at, begin, gains, turns, heads, blocks],
        out_specs=[heads, lse],
        out_shape=[
            jax.ShapeDtypeStruct((count * rows, QUERY_WIDTH), jnp.bfloat16),
            jax.ShapeDtypeStruct((count, KEY_VALUE_HEADS, 1, GROUP * rows), jnp.float32),
        ],
        scratch_shapes=[pltpu.VMEM((keys, rows), jnp.float32)],
        cost_estimate=pl.CostEstimate(
            flops=8 * count * rows * keys * QUERY_WIDTH,
            bytes_accessed=count * (6 * rows * QUERY_WIDTH + 2 * keys * KV_WIDTH),
            transcendentals=count * rows * keys * QUERY_HEADS,
        ),
    )(place, start, gain, tables, qkv, pairs)


def attend_back(offsets, place, start, gain, tables, qkv, pairs, upstream, lse_rows):
    count = len(offsets)
    rows, keys = qkv.shape[0] // count, pairs.shape[0] // count
    at, begin, gains, turns, heads, blocks, lse, sums = row_specs(rows, keys)
    return pl.pallas_call(
        functools.partial(attend_back_kernel, offsets),
        grid=(count, KEY_VALUE_HEADS),
        in_specs=[at, begin, gains, turns, heads, blocks, heads, lse],
        out_specs=[heads, blocks, sums],
        out_shape=[
            jax.ShapeDtypeStruct((count * rows, QUERY_WIDTH), jnp.bfloat16),
            jax.ShapeDtypeStruct((count * keys, KV_WIDTH), jnp.bfloat16),
            jax.ShapeDtypeStruct((HEAD_SIZE, rows), jnp.float32),
        ],
        scratch_shapes=[pltpu.VMEM((keys, rows), jnp.float32)],
        cost_estimate=pl.CostEstimate(
            flops=20 * count * rows * keys * QUERY_WIDTH,
            bytes_accessed=count * (8 * rows * QUERY_WIDTH + 4 * keys * KV_WIDTH),
            transcendentals=count * rows * keys * QUERY_HEADS,
        ),
    )(place, start, gain, tables, qkv, pairs, upstream, lse_rows)


def keys_specs(tokens):
    first = QUERY_WIDTH // PAIR_WIDTH
    return (
        pl.BlockSpec((HEAD_SIZE, 1), lambda h: (0, 0)),
        pl.BlockSpec((2, HEAD_SIZE // 2, tokens), lambda h: (0, 0, 0)),
        pl.BlockSpec((tokens, PAIR_WIDTH), lambda h: (0, first + h)),
        pl.BlockSpec((tokens, PAIR_WIDTH), lambda h: (0, h)),
        pl.BlockSpec((HEAD_SIZE, tokens), lambda h: (0, 0)),
    )


def keys_forward(gain, tables, qkv):
    tokens = qkv.shape[0]
    gains, turns, raw, own, _ = keys_specs(tokens)
    return pl.pallas_call(
        keys_kernel,
        grid=(KEY_VALUE_HEADS,),
        in_specs=[gains, turns, raw],
        out_specs=own,
        out_shape=jax.ShapeDtypeStruct((tokens, KV_WIDTH), jnp.bfloat16),
        cost_estimate=pl.CostEstimate(
            flops=20 * tokens * KV_WIDTH, bytes_accessed=6 * tokens * KV_WIDTH, transcendentals=0
        ),
    )(gain, tables, qkv)


def keys_back(gain, tables, qkv, upstream):
    tokens = qkv.shape[0]
    gains, turns, raw, own, sums = keys_specs(tokens)
    return pl.pallas_call(
        keys_back_kernel,
        grid=(KEY_VALUE_HEADS,),
        in_specs=[gains, turns, raw, own],
        out_specs=[own, sums],
        out_shape=[
            jax.ShapeDtypeStruct((tokens, KV_WIDTH), jnp.bfloat16),
            jax.ShapeDtypeStruct((HEAD_SIZE, tokens), jnp.float32),
        ],
        cost_estimate=pl.CostEstimate(
            flops=40 * tokens * KV_WIDTH, bytes_accessed=10 * tokens * KV_WIDTH, transcendentals=0
        ),
    )(gain, tables, qkv, upstream)


def paired(columns):
    rows = columns.shape[0]
    return (
        columns.reshape(rows, 2, KEY_VALUE_HEADS, HEAD_SIZE)
        .transpose(0, 2, 1, 3)
        .reshape(rows, KV_WIDTH)
    )


def unpaired(columns):
    rows = columns.shape[0]
    return (
        columns.reshape(rows, KEY_VALUE_HEADS, 2, HEAD_SIZE)
        .transpose(0, 2, 1, 3)
        .reshape(rows, KV_WIDTH)
    )


def per_device(
    hidden_in, w_qkv, w_out, w_gate_up, w_down, norm_gains, segment_ids, positions, out_grad
):
    row_count, rows = (hidden_in.shape[0], hidden_in.shape[1])
    dp_count, seq_count = (lax.axis_size("dp"), lax.axis_size("seq"))
    tokens = row_count * rows
    ff_part = FF // dp_count
    place = lax.axis_index("seq")
    orders = bit_orders(seq_count, row_count)
    low = jnp.bfloat16
    split = lambda array: [array[r * rows : (r + 1) * rows] for r in range(row_count)]

    here = place * rows + jnp.arange(rows, dtype=jnp.int32)
    starts = (here[None, :] - positions).reshape(row_count, 1, rows)
    place_one = place.astype(jnp.int32).reshape(1)

    gains_seq = cube_gather_in_order(norm_gains.astype(low))
    gains = in_order(rotate_gather(gains_seq)).reshape(-1).astype(jnp.float32)
    qkv_low = jnp.concatenate(
        [w_qkv[:, :QUERY_WIDTH], paired(w_qkv[:, QUERY_WIDTH:])], axis=1
    ).astype(low)
    qkv_rows = in_order(rotate_gather(qkv_low))
    w_query = lax.all_gather(qkv_rows, "seq", axis=1, tiled=True).reshape(D, -1)
    proj_rows = in_order(rotate_gather(w_out.astype(low)))
    part = lambda start: lax.dynamic_slice_in_dim(w_gate_up, start, ff_part, axis=1)
    gate_cols = exchange_blocks(
        lambda d: jnp.concatenate([part(d * ff_part), part(FF + d * ff_part)], axis=1).astype(low)
    )
    w_proj = lax.all_gather(proj_rows, "seq", axis=1, tiled=True).reshape(QUERY_WIDTH, D)
    w_gate = lax.all_gather(gate_cols, "seq", axis=1, tiled=True).reshape(D, 2 * ff_part)
    w_drop = lax.all_gather(w_down.astype(low), "seq", axis=0, tiled=True)
    grad_low = out_grad.reshape(tokens, D)
    grad_all = jnp.concatenate(line_gather(grad_low), axis=0)

    gain_one = gains[:D]
    gain_two = gains[D : 2 * D]
    gain_query = gains[2 * D : 2 * D + HEAD_SIZE]
    gain_key = gains[2 * D + HEAD_SIZE :]
    inputs = hidden_in.reshape(tokens, D).astype(jnp.float32)
    x_unit, x_scale = normalized_rows(inputs)
    normed = (x_unit * gain_one).astype(low)
    qkv = matmul(normed, w_query)
    tables = rope_tables(positions)
    flat_tables = tables.transpose(1, 2, 0, 3).reshape(2, HEAD_SIZE // 2, tokens)
    query_column, key_column = gain_query[:, None], gain_key[:, None]
    kv_low = keys_forward(key_column, flat_tables, qkv)

    pairs = []
    for r, kv_row in enumerate(split(kv_low)):
        pairs.append(cube_gather(kv_row, orders[r]))
    offsets = tuple(cube_offsets(order) for order in orders)
    pairs = jnp.concatenate(pairs, axis=0)
    attended, lse = attend(
        offsets, place_one, starts, query_column, tables, qkv, pairs
    )
    mixed = inputs + matmul(attended, w_proj)
    y_unit, y_scale = normalized_rows(mixed)
    mixed, y_scale, normed_two = lax.optimization_barrier(
        (mixed, y_scale, (y_unit * gain_two).astype(low))
    )
    normed_all = jnp.concatenate(line_gather(normed_two), axis=0)

    gate_up = matmul(normed_all, w_gate)
    d_hidden = contract_cols(grad_all, w_drop)
    gate, up = gate_up[:, :ff_part], gate_up[:, ff_part:]
    sigmoid_gate = jax.nn.sigmoid(gate)
    silu_gate = gate * sigmoid_gate
    hidden = (silu_gate * up).astype(low)
    d_gate = d_hidden * up * sigmoid_gate * (1.0 + gate * (1.0 - sigmoid_gate))
    d_gate_up = jnp.concatenate([d_gate, d_hidden * silu_gate], axis=-1).astype(low)
    d_partial = contract_cols(d_gate_up, w_gate).astype(low)
    d_normed = line_reduce(d_partial, tokens)
    gate_term = contract_rows(normed_all, d_gate_up).astype(low)
    down_term = contract_rows(hidden, grad_all).astype(low)
    y_partial = matmul(hidden, w_drop).astype(low)
    y_slots = rotate_slots(y_partial, tokens)
    gate_sum = lax.psum_scatter(
        gate_term.reshape(dp_count, D // dp_count, 2 * ff_part),
        "seq", scatter_dimension=1, tiled=True,
    )
    blocks = down_term.reshape(1, seq_count, -1, D)
    half = blocks.shape[2] // 2
    grad_down = jnp.concatenate(
        [
            cube_scatter(part, order)[0]
            for part, order in zip(
                (blocks[:, :, :half], blocks[:, :, half:]), bit_orders(seq_count, 2)
            )
        ]
    )
    gate_own = exchange_blocks(lambda d: lax.dynamic_index_in_dim(gate_sum, d, 0, keepdims=False))
    grad_gate_up = jnp.concatenate(
        [gate_own[d, :, :ff_part] for d in range(dp_count)]
        + [gate_own[d, :, ff_part:] for d in range(dp_count)],
        axis=1,
    ).astype(jnp.float32)

    d_mixed = grad_low.astype(jnp.float32) + normalized_gradient(
        d_normed * gain_two, mixed * y_scale, y_scale
    )
    d_mixed, d_mixed_low, d_normed = lax.optimization_barrier(
        (d_mixed, d_mixed.astype(low), d_normed)
    )
    d_attended = contract_cols(d_mixed_low, w_proj).astype(low)
    out_term = contract_rows(attended, d_mixed_low).astype(low)
    d_q_raw, d_pairs, query_sums = attend_back(
        offsets, place_one, starts, query_column, tables, qkv, pairs, d_attended, lse
    )
    d_kv = []
    for r, d_row in enumerate(jnp.split(d_pairs, row_count)):
        d_kv.append(cube_reduce(d_row, orders[r]))
    out_sum = halves_scatter(out_term.reshape(dp_count, seq_count, -1, D), bit_orders(seq_count, 2))
    grad_out = reduce_blocks(out_sum)

    d_kv_raw, key_sums = keys_back(key_column, flat_tables, qkv, jnp.concatenate(d_kv))
    d_qkv = jnp.concatenate([d_q_raw, d_kv_raw], axis=-1)
    late_mixed, y_scale, d_normed = late((mixed, y_scale, d_normed), d_q_raw)
    d_gain_two = jnp.sum(d_normed * (late_mixed * y_scale), axis=0)
    qkv_term = contract_rows(normed, d_qkv).astype(low)
    d_first = contract_cols(d_qkv, w_query)
    d_gain_one = jnp.sum(d_first * x_unit, axis=0)
    d_inputs = late(d_mixed, qkv_term) + normalized_gradient(d_first * gain_one, x_unit, x_scale)
    in_grad = d_inputs.astype(low).reshape(row_count, rows, D)
    gain_term = jnp.concatenate(
        [d_gain_one, d_gain_two, jnp.sum(query_sums, axis=1), jnp.sum(key_sums, axis=1)]
    ).astype(low)
    qkv_rows, gain_count = D // dp_count // seq_count, norm_gains.shape[0]
    block = jnp.concatenate(
        [
            qkv_term.reshape(dp_count, seq_count, qkv_rows, -1),
            jnp.pad(
                gain_term.reshape(dp_count, seq_count, 1, gain_count),
                ((0, 0), (0, 0), (0, 7), (0, QUERY_WIDTH + KV_WIDTH - gain_count)),
            ),
        ],
        axis=2,
    )
    qkv_sum = halves_scatter(block, bit_orders(seq_count, 2))
    y_slots, mixed = late((y_slots, mixed), qkv_term)
    block_out = (mixed + added(y_slots)).astype(low).reshape(row_count, rows, D)
    qkv_own = reduce_blocks(qkv_sum)
    grad_gains = qkv_own[qkv_rows, :gain_count]
    grad_qkv = jnp.concatenate(
        [qkv_own[:qkv_rows, :QUERY_WIDTH], unpaired(qkv_own[:qkv_rows, QUERY_WIDTH:])], axis=1
    )
    return (
        block_out, in_grad, grad_qkv, grad_out, grad_gate_up, grad_down, grad_gains
    )


def late(values, anchor):
    return lax.optimization_barrier((values, anchor))[0]


def solution(mesh):
    both = ("dp", "seq")
    return jax.shard_map(
        per_device,
        mesh=mesh,
        in_specs=(
            P("dp", "seq", None),
            P(both, None),
            P(both, None),
            P(both, None),
            P(both, None),
            P(both),
            P("dp", "seq"),
            P("dp", "seq"),
            P("dp", "seq", None),
        ),
        out_specs=(
            P("dp", "seq", None),
            P("dp", "seq", None),
            P(both, None),
            P(both, None),
            P(both, None),
            P(both, None),
            P(both),
        ),
        check_vma=False,
    )
```

time: 1110 us -> 840 us (0.76)
  waiting for transfers between devices: 541 us -> 397 us
  blocking collectives: 92.5 us -> 0 us
  local copies, waits for them, and re-layouts: 111 us -> 57.8 us
  starting transfers between devices: 75.4 us -> 114 us
  matrix products: 178 us -> 140 us
    ppermute x42 -> x24, waiting for transfers between devices: 297 us -> 130 us  [shifted(): lax.ppermute(piece, 'dp', [(i, (i + shift) % count) for i in range(count)])]
    ppermute x0 -> x18, waiting for transfers between devices: none -> 147 us  [the longest x3 76.1 us: line_reduce(): up = lax.ppermute(up, 'dp', [(i, i + 1) for i in range(hop)])]
    reduce_scatter x1, waiting for transfers between devices: 114 us -> 0.01 us  [per_device(): lax.psum_scatter(gate_term.reshape(dp_count, D // dp_count, 2 * ff_part),...]
    unnamed x1 -> x0, blocking collectives: 92.5 us -> none
    reduce_scatter x2 -> x0, waiting for transfers between devices: 81 us -> none  [the longest x1 70.1 us: per_device(): lax.psum_scatter(qkv_term.reshape(dp_count, D // dp_count, QUERY_WIDTH +...]
    ppermute x15 -> x33, waiting for transfers between devices: 47.6 us -> 120 us  [crossed(): return lax.ppermute(piece, 'seq', [(i, i ^ bit) for i in range(count)])]
    ppermute x0 -> x18, starting transfers between devices: none -> 52.6 us  [the longest x6 22.6 us: line_gather(): lax.ppermute(down, 'dp', [(i, i - 1) for i in range(1, count + 1 - hop)])]
    ppermute x42 -> x24, starting transfers between devices: 63 us -> 36.2 us  [shifted(): lax.ppermute(piece, 'dp', [(i, (i + shift) % count) for i in range(count)])]
  transfers between devices with their start and end apart: 65 -> 80, of which waited for: 34 -> 37; matrix products, arithmetic and copies ran while one was open for 24% -> 19% of each run, Pallas kernels for 3% -> 6%
where the time goes in v2:
time: 840 us; the launch traced here: 826 us
  waiting for transfers between devices  397 us (47%)
  matrix products  140 us (17%)
  starting transfers between devices  114 us (14%)
  local copies, waits for them, and re-layouts  57.8 us (7%)
  other arithmetic  56.2 us (7%)
  Pallas kernels  45.8 us (5%)
  between operations  15.6 us (2%)
    ppermute x24, waiting for transfers between devices, shifted(): lax.ppermute(piece, 'dp', [(i, (i + shift) % count) for i in range(count)])  130 us
    ppermute x33, waiting for transfers between devices, crossed(): return lax.ppermute(piece, 'seq', [(i, i ^ bit) for i in range(count)])  120 us
    ppermute x3, waiting for transfers between devices, line_reduce(): up = lax.ppermute(up, 'dp', [(i, i + 1) for i in range(hop)])  76.1 us
    ppermute x6, waiting for transfers between devices, line_gather(): lax.ppermute(down, 'dp', [(i, i - 1) for i in range(1, count + 1 - hop)])  67.6 us
    dot_general x4, matrix products, contract_cols(): lax.dot_general(left, right, (((1,), (1,)), ((), ())), preferred_element_...  52.7 us
    dot_general x4, matrix products, matmul(): return jnp.dot(left, right, preferred_element_type=jnp.float32)  46.2 us
    dot_general x4, matrix products, contract_rows(): lax.dot_general(left, right, (((0,), (0,)), ((), ())), preferred_element_...  40.9 us
    ppermute x24, starting transfers between devices, shifted(): lax.ppermute(piece, 'dp', [(i, (i + shift) % count) for i in range(count)])  36.2 us
  transfers between devices with their start and end apart: 80, of which 37 were waited for; matrix products, arithmetic and copies ran while one was open for 19% of the time, Pallas kernels for 6%

profile of v2, /device:TPU:14, one launch (start us, length us, event | category | flops | bytes accessed | tf_op | source)
XLA Modules:
  0.0 826.0 jit_solution(12020840978710209820)
XLA Ops:
  16.4 12.7 %collective-permute-done.6 = bf16[64,1920]{1,0:T(8,128)(2,1)S(1)} collective-permute-done((bf16[64,1920]{1,0:T(8,128)(2,1)S(1)}, bf16[64,1920]{1,0:T(8,128)(2,1)S(1)}, u32[]{:S(2)}, u32[]{:S(2)}) %collective-permute-start.6) | collective-permute-done | bytes 245792 | tf_op jit(solution)/shard_map/ppermute | solution.py:62
  38.8 10.6 %collective-permute-done.15 = bf16[40,2048]{1,0:T(8,128)(2,1)S(1)} collective-permute-done((bf16[40,2048]{1,0:T(8,128)(2,1)S(1)}, bf16[40,2048]{1,0:T(8,128)(2,1)S(1)}, u32[]{:S(2)}, u32[]{:S(2)}) %collective-permute-start.15) | collective-permute-done | bytes 163872 | tf_op jit(solution)/shard_map/ppermute | solution.py:62
  68.3 20.8 %collective-permute-done.25 = bf16[64,4096]{1,0:T(8,128)(2,1)S(1)} collective-permute-done((bf16[64,4096]{1,0:T(8,128)(2,1)S(1)}, bf16[64,4096]{1,0:T(8,128)(2,1)S(1)}, u32[]{:S(2)}, u32[]{:S(2)}) %collective-permute-start.25) | collective-permute-done | bytes 524320 | tf_op jit(solution)/shard_map/ppermute | solution.py:62
  89.1 11.1 %collective-permute-done.26 = bf16[64,4096]{1,0:T(8,128)(2,1)S(1)} collective-permute-done((bf16[64,4096]{1,0:T(8,128)(2,1)S(1)}, bf16[64,4096]{1,0:T(8,128)(2,1)S(1)}, u32[]{:S(2)}, u32[]{:S(2)}) %collective-permute-start.26) | collective-permute-done | bytes 524320 | tf_op jit(solution)/shard_map/ppermute | solution.py:62
  142.9 11.2 %collective-permute-done.10 = bf16[256,640]{1,0:T(8,128)(2,1)S(1)} collective-permute-done((bf16[256,640]{1,0:T(8,128)(2,1)S(1)}, bf16[256,640]{1,0:T(8,128)(2,1)S(1)}, u32[]{:S(2)}, u32[]{:S(2)}) %collective-permute-start.10) | collective-permute-done | bytes 327712 | tf_op jit(solution)/shard_map/ppermute | solution.py:148
  180.2 15.6 %shard_map.136 = (bf16[256,1280]{1,0:T(8,128)(2,1)}, f32[2,5,1,512]{3,2,1,0:T(1,128)}) custom-call(s32[1]{0:T(128)} %bitcast.1.place_ref, s32[2,1,128]{2,1,0:T(1,128)} %bitcast.286, f32[64,1]{1,0:T(8,128)} %copy.46.gain_ref, f32[2,2,32,128]{3,2,1,0:T(8,128)} %get-tuple-element.102.table_ref, f32[256,1920]{1,0:T(8,128)} %fusion.67.kv_ref.q_ref, ...), custom_call_target="tpu_custom_call" | custom-call | flops 2684354560 | bytes 4587520 | tf_op jit(solution)/shard_map/pallas_call | solution.py:367
  211.9 17.4 %collective-permute-done.19 = bf16[256,2048]{1,0:T(8,128)(2,1)S(1)} collective-permute-done((bf16[256,2048]{1,0:T(8,128)(2,1)S(1)}, bf16[256,2048]{1,0:T(8,128)(2,1)S(1)}, u32[]{:S(2)}, u32[]{:S(2)}) %collective-permute-start.19) | collective-permute-done | bytes 1048608 | tf_op jit(solution)/shard_map/ppermute | solution.py:75
  240.4 31.9 %collective-permute-done.20 = bf16[256,2048]{1,0:T(8,128)(2,1)S(1)} collective-permute-done((bf16[256,2048]{1,0:T(8,128)(2,1)S(1)}, bf16[256,2048]{1,0:T(8,128)(2,1)S(1)}, u32[]{:S(2)}, u32[]{:S(2)}) %collective-permute-start.20) | collective-permute-done | bytes 1048608 | tf_op jit(solution)/shard_map/ppermute | solution.py:75
  280.9 18.2 %collective-permute-done.21 = bf16[256,2048]{1,0:T(8,128)(2,1)S(1)} collective-permute-done((bf16[256,2048]{1,0:T(8,128)(2,1)S(1)}, bf16[256,2048]{1,0:T(8,128)(2,1)S(1)}, u32[]{:S(2)}, u32[]{:S(2)}) %collective-permute-start.21) | collective-permute-done | bytes 1048608 | tf_op jit(solution)/shard_map/ppermute | solution.py:75
  301.3 23.3 %fusion.12 = f32[1024,4096]{1,0:T(8,128)} fusion(bf16[2048,4096]{1,0:T(8,128)(2,1)} %bitcast.289, bf16[256,2048]{1,0:T(8,128)(2,1)} %broadcast_select_fusion.1, bf16[256,2048]{1,0:T(8,128)(2,1)} %broadcast_select_fusion.3, bf16[256,2048]{1,0:T(8,128)(2,1)} %broadcast_select_fusion.5, bf16[256,2048]{1,0:T(8,128)(2,1)S(1)} %multiply_convert_fusion.4), kind=kOutput, calls=%fused_computation.102 | convolution fusion | flops 17196646400 | bytes 37748736 | tf_op jit(solution)/shard_map/dot_general | solution.py:45
  324.7 19.9 %multiply_convert_fusion.1 = (bf16[1024,2048]{1,0:T(8,128)(2,1)}, bf16[1024,2048]{1,0:T(8,128)(2,1)}, bf16[1024,2048]{1,0:T(8,128)(2,1)}) fusion(f32[1024,4096]{1,0:T(8,128)} %fusion.12, bf16[2048,2048]{1,0:T(8,128)(2,1)} %all-gather.11.cloned.1.call-done, bf16[256,2048]{1,0:T(8,128)(2,1)S(1)} %copy-done.29, bf16[256,2048]{1,0:T(8,128)(2,1)S(1)} %copy-done.28, ...), kind=kOutput, calls=%fused_computation.6 | convolution fusion | flops 8638169088 | bytes 41943040 | tf_op jit(solution)/shard_map/dot_general | solution.py:55
  344.6 24.9 %convolution_convert_fusion = bf16[2048,4096]{1,0:T(8,128)(2,1)} fusion(bf16[1024,2048]{1,0:T(8,128)(2,1)} %get-tuple-element.58, bf16[1024,2048]{1,0:T(8,128)(2,1)} %get-tuple-element.57, bf16[256,2048]{1,0:T(8,128)(2,1)} %broadcast_select_fusion.1, bf16[256,2048]{1,0:T(8,128)(2,1)} %broadcast_select_fusion.3, ...), kind=kOutput, calls=%fused_computation.2 | convolution fusion | flops 17221812224 | bytes 29360128 | tf_op jit(solution)/shard_map/dot_general | solution.py:49
  369.5 22.7 %fusion.4 = bf16[1024,2048]{1,0:T(8,128)(2,1)} fusion(bf16[2048,4096]{1,0:T(8,128)(2,1)} %bitcast.290, bf16[1024,2048]{1,0:T(8,128)(2,1)} %get-tuple-element.58, bf16[1024,2048]{1,0:T(8,128)(2,1)S(1)} %copy-done.44), kind=kOutput, calls=%fused_computation.20 | convolution fusion | flops 17198743552 | bytes 29360128 | tf_op jit(solution)/shard_map/dot_general | solution.py:55
  392.2 10.6 %convolution_convert_fusion.1 = bf16[2048,2048]{1,0:T(8,128)(2,1)S(1)} fusion(bf16[1024,2048]{1,0:T(8,128)(2,1)S(1)} %copy-done.42, bf16[256,2048]{1,0:T(8,128)(2,1)S(1)} %copy-done.29, bf16[256,2048]{1,0:T(8,128)(2,1)S(1)} %copy-done.28, bf16[256,2048]{1,0:T(8,128)(2,1)S(1)} %copy-done.30, bf16[256,2048]{1,0:T(8,128)(2,1)} %bitcast.28), kind=kOutput, calls=%fused_computation.10 | convolution fusion | flops 8610906112 | bytes 16777216 | tf_op jit(solution)/shard_map/dot_general | solution.py:49
  411.6 11.6 %convolution_convert_fusion.4 = bf16[1024,2048]{1,0:T(8,128)(2,1)S(1)} fusion(bf16[1024,2048]{1,0:T(8,128)(2,1)S(1)} %copy-done.43, bf16[2048,2048]{1,0:T(8,128)(2,1)} %all-gather.11.cloned.1.call-done), kind=kOutput, calls=%fused_computation.21 | convolution fusion | flops 8592031744 | bytes 16777216 | tf_op jit(solution)/shard_map/dot_general | solution.py:45
  423.2 13.8 %collective-permute-done.36 = bf16[256,2048]{1,0:T(8,128)(2,1)S(1)} collective-permute-done((bf16[256,2048]{1,0:T(8,128)(2,1)S(1)}, bf16[256,2048]{1,0:T(8,128)(2,1)S(1)}, u32[]{:S(2)}, u32[]{:S(2)}) %collective-permute-start.36) | collective-permute-done | bytes 1048608 | tf_op jit(solution)/shard_map/ppermute | solution.py:100
  454.2 58.1 %collective-permute-done.37 = bf16[256,2048]{1,0:T(8,128)(2,1)S(1)} collective-permute-done((bf16[256,2048]{1,0:T(8,128)(2,1)S(1)}, bf16[256,2048]{1,0:T(8,128)(2,1)S(1)}, u32[]{:S(2)}, u32[]{:S(2)}) %collective-permute-start.37) | collective-permute-done | bytes 1048608 | tf_op jit(solution)/shard_map/ppermute | solution.py:100
  523.9 24.0 %collective-permute-done.70 = bf16[1,2,128,2048]{3,2,1,0:T(8,128)(2,1)S(1)} collective-permute-done((bf16[1,2,128,2048]{3,2,1,0:T(8,128)(2,1)S(1)}, bf16[1,2,128,2048]{3,2,1,0:T(8,128)(2,1)S(1)}, u32[]{:S(2)}, u32[]{:S(2)}) %collective-permute-start.70) | collective-permute-done | bytes 1048608 | tf_op jit(solution)/shard_map/ppermute | solution.py:148
  567.7 21.2 %shard_map.137 = (bf16[256,1280]{1,0:T(8,128)(2,1)}, bf16[2048,640]{1,0:T(8,128)(2,1)}, f32[64,128]{1,0:T(8,128)}) custom-call(s32[1]{0:T(128)} %bitcast.1.place_ref, s32[2,1,128]{2,1,0:T(1,128)} %bitcast.287, f32[64,1]{1,0:T(8,128)} %copy.46.gain_ref, f32[2,2,32,128]{3,2,1,0:T(8,128)} %get-tuple-element.102.table_ref, f32[256,1920]{1,0:T(8,128)} %fusion.67.kv_ref.q_ref, ...), custom_call_target="tpu_custom_call" | custom-call | flops 6710886400 | bytes 7864320 | tf_op jit(solution)/shard_map/pallas_call | solution.py:389
  610.3 10.0 %collective-permute-done.74 = bf16[1,1,128,2048]{3,2,1,0:T(8,128)(2,1)S(1)} collective-permute-done((bf16[1,1,128,2048]{3,2,1,0:T(8,128)(2,1)S(1)}, bf16[1,1,128,2048]{3,2,1,0:T(8,128)(2,1)S(1)}, u32[]{:S(2)}, u32[]{:S(2)}) %collective-permute-start.74) | collective-permute-done | bytes 524320 | tf_op jit(solution)/shard_map/ppermute | solution.py:148
  680.0 13.0 %collective-permute-done.61 = bf16[2,2,40,2048]{3,2,1,0:T(8,128)(2,1)S(1)} collective-permute-done((bf16[2,2,40,2048]{3,2,1,0:T(8,128)(2,1)S(1)}, bf16[2,2,40,2048]{3,2,1,0:T(8,128)(2,1)S(1)}, u32[]{:S(2)}, u32[]{:S(2)}) %collective-permute-start.61) | collective-permute-done | bytes 655392 | tf_op jit(solution)/shard_map/ppermute | solution.py:148
  710.7 19.1 %collective-permute-done.52 = bf16[2,2,72,1920]{3,2,1,0:T(8,128)(2,1)S(1)} collective-permute-done((bf16[2,2,72,1920]{3,2,1,0:T(8,128)(2,1)S(1)}, bf16[2,2,72,1920]{3,2,1,0:T(8,128)(2,1)S(1)}, u32[]{:S(2)}, u32[]{:S(2)}) %collective-permute-start.52) | collective-permute-done | bytes 1105952 | tf_op jit(solution)/shard_map/ppermute | solution.py:148
  752.0 28.8 %collective-permute-done.54 = bf16[72,1920]{1,0:T(8,128)(2,1)} collective-permute-done((bf16[72,1920]{1,0:T(8,128)(2,1)}, bf16[72,1920]{1,0:T(8,128)(2,1)}, u32[]{:S(2)}, u32[]{:S(2)}) %collective-permute-start.54) | collective-permute-done | bytes 276512 | tf_op jit(solution)/shard_map/ppermute | solution.py:62
  790.5 16.4 %collective-permute-done.67 = bf16[64,4096]{1,0:T(8,128)(2,1)S(1)} collective-permute-done((bf16[64,4096]{1,0:T(8,128)(2,1)S(1)}, bf16[64,4096]{1,0:T(8,128)(2,1)S(1)}, u32[]{:S(2)}, u32[]{:S(2)}) %collective-permute-start.67) | collective-permute-done | bytes 524320 | tf_op jit(solution)/shard_map/ppermute | solution.py:62
  (440 shorter events, 343.4 us)
Async XLA Ops:
  7.2 114.4 %all-gather.5.cloned.1.call-start = ((), (), s32[]{:S(2)}) async-start(), calls=%async_computation.1 | async-start | bytes 8847360 | tf_op jit(solution)/shard_map/all_gather | solution.py:492
  34.7 161.1 %all-gather.7.cloned.1.call-start = ((), (), s32[]{:S(2)}) async-start(), calls=%async_computation.2 | async-start | bytes 5898240 | tf_op jit(solution)/shard_map/all_gather | solution.py:498
  50.5 250.8 %all-gather.9.cloned.1.call-start = ((), (), s32[]{:S(2)}) async-start(), calls=%async_computation.3 | async-start | bytes 18874368 | tf_op jit(solution)/shard_map/all_gather | solution.py:499
  56.9 43.4 %collective-permute-start.26 = (bf16[64,4096]{1,0:T(8,128)(2,1)S(1)}, bf16[64,4096]{1,0:T(8,128)(2,1)S(1)}, u32[]{:S(2)}, u32[]{:S(2)}) collective-permute-start(bf16[64,4096]{1,0:T(8,128)(2,1)S(1)} %pad_maximum_fusion.17), channel_id=1, source_target_pairs={{0,8},{8,16},{16,24},{24,0},{1,9},{9,17},{17,25},{25,1},{2,10},{10... | collective-permute-start | bytes 1572872 | tf_op jit(solution)/shard_map/ppermute | solution.py:62
  102.0 222.7 %all-gather.11.cloned.1.call-start = ((), (), s32[]{:S(2)}) async-start(), calls=%async_computation.4 | async-start | bytes 9437184 | tf_op jit(solution)/shard_map/all_gather | solution.py:500
  103.9 645.1 %reduce-scatter.2.cloned.1.call-start = ((), (), s32[]{:S(2)}) async-start(), calls=%async_computation.5 | async-start | bytes 18874368 | tf_op jit(solution)/shard_map/reduce_scatter | solution.py:546
  162.8 46.6 %collective-permute-start.32 = (bf16[256,2048]{1,0:T(8,128)(2,1)}, bf16[256,2048]{1,0:T(8,128)(2,1)}, u32[]{:S(2)}, u32[]{:S(2)}) collective-permute-start(bf16[256,2048]{1,0:T(8,128)(2,1)} %collective-permute-done.31), channel_id=1, source_target_pairs={{8,0},{16,8},{9,1},{17,9},{10,2},{18,10},{11,3},{19,11},{12,4},{20... | collective-permute-start | bytes 3145736 | tf_op jit(solution)/shard_map/ppermute | solution.py:75
  209.3 67.5 %collective-permute-start.33 = (bf16[256,2048]{1,0:T(8,128)(2,1)}, bf16[256,2048]{1,0:T(8,128)(2,1)S(1)}, u32[]{:S(2)}, u32[]{:S(2)}) collective-permute-start(bf16[256,2048]{1,0:T(8,128)(2,1)} %collective-permute-done.32), channel_id=1, source_target_pairs={{8,0},{9,1},{10,2},{11,3},{12,4},{13,5},{14,6},{15,7}} | collective-permute-start | bytes 3145736 | tf_op jit(solution)/shard_map/ppermute | solution.py:75
  229.3 43.0 %collective-permute-start.20 = (bf16[256,2048]{1,0:T(8,128)(2,1)S(1)}, bf16[256,2048]{1,0:T(8,128)(2,1)S(1)}, u32[]{:S(2)}, u32[]{:S(2)}) collective-permute-start(bf16[256,2048]{1,0:T(8,128)(2,1)S(1)} %collective-permute-done.19), channel_id=1, source_target_pairs={{8,0},{16,8},{9,1},{17,9},{10,2},{18,10},{11,3},{19,11},{12,4},{20... | collective-permute-start | bytes 3145736 | tf_op jit(solution)/shard_map/ppermute | solution.py:75
  234.8 44.4 %collective-permute-start.22 = (bf16[256,2048]{1,0:T(8,128)(2,1)S(1)}, bf16[256,2048]{1,0:T(8,128)(2,1)S(1)}, u32[]{:S(2)}, u32[]{:S(2)}) collective-permute-start(bf16[256,2048]{1,0:T(8,128)(2,1)S(1)} %collective-permute-done.18), channel_id=1, source_target_pairs={{8,16},{16,24},{9,17},{17,25},{10,18},{18,26},{11,19},{19,27},{12,... | collective-permute-start | bytes 3145736 | tf_op jit(solution)/shard_map/ppermute | solution.py:74
  405.2 42.3 %collective-permute-start.69 = (bf16[1,4,128,2048]{3,2,1,0:T(8,128)(2,1)}, bf16[1,4,128,2048]{3,2,1,0:T(8,128)(2,1)}, u32[]{:S(2)}, u32[]{:S(2)}) collective-permute-start(bf16[1,4,128,2048]{3,2,1,0:T(8,128)(2,1)} %dynamic-slice_bitcast_fusion.3), channel_id=1, source_target_pairs={{0,1},{1,0},{2,3},{3,2},{4,5},{5,4},{6,7},{7,6},{8,9},{9,8},{10,11... | collective-permute-start | bytes 6291464 | tf_op jit(solution)/shard_map/ppermute | solution.py:148
  407.4 111.0 %collective-permute-start.72 = (bf16[1,4,128,2048]{3,2,1,0:T(8,128)(2,1)S(1)}, bf16[1,4,128,2048]{3,2,1,0:T(8,128)(2,1)}, u32[]{:S(2)}, u32[]{:S(2)}) collective-permute-start(bf16[1,4,128,2048]{3,2,1,0:T(8,128)(2,1)S(1)} %dynamic-slice_bitcast_fusion.2), channel_id=1, source_target_pairs={{0,1},{1,0},{2,3},{3,2},{4,5},{5,4},{6,7},{7,6},{8,9},{9,8},{10,11... | collective-permute-start | bytes 6291464 | tf_op jit(solution)/shard_map/ppermute | solution.py:148
  437.6 74.7 %collective-permute-start.37 = (bf16[256,2048]{1,0:T(8,128)(2,1)S(1)}, bf16[256,2048]{1,0:T(8,128)(2,1)S(1)}, u32[]{:S(2)}, u32[]{:S(2)}) collective-permute-start(bf16[256,2048]{1,0:T(8,128)(2,1)S(1)} %get-tuple-element.68), channel_id=1, source_target_pairs={{0,8},{8,16},{1,9},{9,17},{2,10},{10,18},{3,11},{11,19},{4,12},{12... | collective-permute-start | bytes 3145736 | tf_op jit(solution)/shard_map/ppermute | solution.py:100
  443.9 69.0 %collective-permute-start.40 = (bf16[256,2048]{1,0:T(8,128)(2,1)S(1)}, bf16[256,2048]{1,0:T(8,128)(2,1)S(1)}, u32[]{:S(2)}, u32[]{:S(2)}) collective-permute-start(bf16[256,2048]{1,0:T(8,128)(2,1)S(1)} %get-tuple-element.69), channel_id=1, source_target_pairs={{16,8},{24,16},{17,9},{25,17},{18,10},{26,18},{19,11},{27,19},{20,... | collective-permute-start | bytes 3145736 | tf_op jit(solution)/shard_map/ppermute | solution.py:101
  447.5 219.7 %collective-permute-start.27 = (bf16[256,2048]{1,0:T(8,128)(2,1)}, bf16[256,2048]{1,0:T(8,128)(2,1)}, u32[]{:S(2)}, u32[]{:S(2)}) collective-permute-start(bf16[256,2048]{1,0:T(8,128)(2,1)} %get-tuple-element.74), channel_id=1, source_target_pairs={{0,24},{8,0},{16,8},{24,16},{1,25},{9,1},{17,9},{25,17},{2,26},{10... | collective-permute-start | bytes 3145736 | tf_op jit(solution)/shard_map/ppermute | solution.py:62
  447.5 220.3 %collective-permute-start.28 = (bf16[256,2048]{1,0:T(8,128)(2,1)}, bf16[256,2048]{1,0:T(8,128)(2,1)}, u32[]{:S(2)}, u32[]{:S(2)}) collective-permute-start(bf16[256,2048]{1,0:T(8,128)(2,1)} %get-tuple-element.73), channel_id=1, source_target_pairs={{0,16},{8,24},{16,0},{24,8},{1,17},{9,25},{17,1},{25,9},{2,18},{10... | collective-permute-start | bytes 3145736 | tf_op jit(solution)/shard_map/ppermute | solution.py:62
  513.8 42.3 %collective-permute-start.38 = (bf16[256,2048]{1,0:T(8,128)(2,1)S(1)}, bf16[256,2048]{1,0:T(8,128)(2,1)S(1)}, u32[]{:S(2)}, u32[]{:S(2)}) collective-permute-start(bf16[256,2048]{1,0:T(8,128)(2,1)S(1)} %get-tuple-element.66), channel_id=1, source_target_pairs={{0,8},{8,16},{16,24},{1,9},{9,17},{17,25},{2,10},{10,18},{18,26},{... | collective-permute-start | bytes 3145736 | tf_op jit(solution)/shard_map/ppermute | solution.py:100
  518.4 42.0 %collective-permute-start.41 = (bf16[256,2048]{1,0:T(8,128)(2,1)S(1)}, bf16[256,2048]{1,0:T(8,128)(2,1)S(1)}, u32[]{:S(2)}, u32[]{:S(2)}) collective-permute-start(bf16[256,2048]{1,0:T(8,128)(2,1)S(1)} %get-tuple-element.67), channel_id=1, source_target_pairs={{8,0},{16,8},{24,16},{9,1},{17,9},{25,17},{10,2},{18,10},{26,18},{... | collective-permute-start | bytes 3145736 | tf_op jit(solution)/shard_map/ppermute | solution.py:101
  548.0 49.7 %collective-permute-start.73 = (bf16[1,2,128,2048]{3,2,1,0:T(8,128)(2,1)}, bf16[1,2,128,2048]{3,2,1,0:T(8,128)(2,1)}, u32[]{:S(2)}, u32[]{:S(2)}) collective-permute-start(bf16[1,2,128,2048]{3,2,1,0:T(8,128)(2,1)} %fusion.10), channel_id=1, source_target_pairs={{0,2},{1,3},{2,0},{3,1},{4,6},{5,7},{6,4},{7,5},{8,10},{9,11},{10,... | collective-permute-start | bytes 3145736 | tf_op jit(solution)/shard_map/ppermute | solution.py:148
  556.0 49.4 %collective-permute-start.71 = (bf16[1,1,128,2048]{3,2,1,0:T(8,128)(2,1)}, bf16[1,1,128,2048]{3,2,1,0:T(8,128)(2,1)}, u32[]{:S(2)}, u32[]{:S(2)}) collective-permute-start(bf16[1,1,128,2048]{3,2,1,0:T(8,128)(2,1)} %dynamic-slice_convert_fusion.9), channel_id=1, source_target_pairs={{0,2},{1,3},{2,0},{3,1},{4,6},{5,7},{6,4},{7,5},{8,10},{9,11},{10,... | collective-permute-start | bytes 1572872 | tf_op jit(solution)/shard_map/ppermute | solution.py:148
  607.3 60.5 %collective-permute-start.29 = (bf16[256,2048]{1,0:T(8,128)(2,1)}, bf16[256,2048]{1,0:T(8,128)(2,1)}, u32[]{:S(2)}, u32[]{:S(2)}) collective-permute-start(bf16[256,2048]{1,0:T(8,128)(2,1)} %get-tuple-element.72), channel_id=1, source_target_pairs={{0,8},{8,16},{16,24},{24,0},{1,9},{9,17},{17,25},{25,1},{2,10},{10... | collective-permute-start | bytes 3145736 | tf_op jit(solution)/shard_map/ppermute | solution.py:62
  626.4 46.9 %collective-permute-start.60 = (bf16[2,4,40,2048]{3,2,1,0:T(8,128)(2,1)}, bf16[2,4,40,2048]{3,2,1,0:T(8,128)(2,1)}, u32[]{:S(2)}, u32[]{:S(2)}) collective-permute-start(bf16[2,4,40,2048]{3,2,1,0:T(8,128)(2,1)} %dynamic-slice_bitcast_fusion.4), channel_id=1, source_target_pairs={{0,1},{1,0},{2,3},{3,2},{4,5},{5,4},{6,7},{7,6},{8,9},{9,8},{10,11... | collective-permute-start | bytes 3932168 | tf_op jit(solution)/shard_map/ppermute | solution.py:148
  744.9 38.8 %collective-permute-start.55 = (bf16[72,1920]{1,0:T(8,128)(2,1)}, bf16[72,1920]{1,0:T(8,128)(2,1)}, u32[]{:S(2)}, u32[]{:S(2)}) collective-permute-start(bf16[72,1920]{1,0:T(8,128)(2,1)} %get-tuple-element.92), channel_id=1, source_target_pairs={{0,16},{8,24},{16,0},{24,8},{1,17},{9,25},{17,1},{25,9},{2,18},{10... | collective-permute-start | bytes 829448 | tf_op jit(solution)/shard_map/ppermute | solution.py:62
  750.5 40.0 %collective-permute-start.66 = (bf16[64,4096]{1,0:T(8,128)(2,1)S(1)}, bf16[64,4096]{1,0:T(8,128)(2,1)S(1)}, u32[]{:S(2)}, u32[]{:S(2)}) collective-permute-start(bf16[64,4096]{1,0:T(8,128)(2,1)S(1)} %get-tuple-element.90), channel_id=1, source_target_pairs={{0,24},{8,0},{16,8},{24,16},{1,25},{9,1},{17,9},{25,17},{2,26},{10... | collective-permute-start | bytes 1572872 | tf_op jit(solution)/shard_map/ppermute | solution.py:62
  (105 other events, 1741.8 us)
Sparse Core Ops, SparseCore 0:
  34.8 52.0 all-gather.4
  89.5 41.0 all-gather.6
  133.0 96.2 all-gather.8
  231.1 54.2 all-gather.10
  407.5 151.3 reduce-scatter.1
